TPU v7x, 1024 devices: a whole 8x8x8 slice. The times are simulated.
1024 devices in a mesh: wide: 64 (over y, x), narrow: 4 (over z_lo, core), rep: 4 (over z_hi).
Axes of the slice: x: 8, y: 8, z: 8 (z_hi: 4, z_lo: 2; z = z_hi * 2 + z_lo), core: 2. Of those that a mesh axis runs over, the one named last changes fastest.
Arguments:
- queries: bfloat16 [65536, 2048], P(('rep', 'wide'), 'narrow'), parts along dimension 0, may hold values from -20 to 20
- key_rows: bfloat16 [65536, 512], P(('rep', 'wide'), 'narrow'), parts along dimension 0, may hold values from -20 to 20
- value_rows: bfloat16 [65536, 512], P(('rep', 'wide'), 'narrow'), parts along dimension 0, may hold values from -20 to 20
- residual: bfloat16 [65536, 4096], P(('rep', 'wide', 'narrow')), parts along dimension 0, may hold values from -9 to 9
- out_weight: bfloat16 [2048, 4096], P('narrow'), may hold values from -0.125 to 0.125
- norm_gain: bfloat16 [4096], replicated, may hold values from 0.099609375 to 1.8984375
- span_map: int32 [64], replicated, may hold values from 0 to 63, each once
- segments: int32 [256, 128], P(('rep', 'wide')), parts along dimension 0, may hold values from 0 to 8, as said below
- row_owner: int32 [65536, 1], P(('rep', 'wide', 'narrow')), parts along dimension 0, may hold values from 0 to 63; in each aligned block of 64 rows (0 to 63, 64 to 127, ...) at most 2 rows name the same one
Outputs:
- hidden: bfloat16 [65536, 4096], P(('rep', 'wide', 'narrow')), parts along dimension 0
- ffn_in: bfloat16 [256, 4, 64, 2, 4096], P(('rep', 'wide'), 'narrow'), parts along dimension 0
There are 4 independent parts, one for each index of `rep`. A program takes and returns all parts, laid end to end along the dimension named above; an argument that names none is the same for every part. Nothing has to cross between parts.
Inputs may be any that keep to these rules, and one draw needn't show every extreme that they name: `segments`: in each token block the short document numbers start at 0, never fall, and rise by at most one from a row to the next; short rows 0 and 1 lie in the same document; some token block reaches the largest number. `row_owner`: within each aligned block of 64 rows no owner is named by more than 2 rows; in some blocks an owner is named by exactly 2 rows.
All inputs are finite; a program needn't handle non-finite values.
Results may differ from a plain program's by a relative error of at most 0.012.
Values may be sent and summed in bfloat16 or wider, within the bound.
No kernel may reach another device: no remote copies, remote signals or barrier semaphores. Data moves between devices by JAX's collectives and lax.ppermute only.
A program may use at most 64 MiB of HBM per device.

v0:
```python
import jax
import jax.numpy as jnp
from jax import lax
from jax.sharding import PartitionSpec as P

HEAD = 128
LONG_DEV = 128


def sent_together(arrays, axis, dim, along):
    ends, at = ([], 0)
    for a in arrays[:-1]:
        at += a.shape[along]
        ends.append(at)
    both = jnp.concatenate(arrays, axis=along)
    return tuple(jnp.split(lax.all_gather(both, axis, axis=dim, tiled=True), ends, axis=along))


def in_blocks(shard, dim, devices):
    dims = shard.shape
    parts = shard.reshape(*dims[:dim], devices, dims[dim] // devices, *dims[dim + 1 :])
    return jnp.moveaxis(parts, dim, 0)


def sum_at_owner(shard, axis, dim):
    parts = in_blocks(shard, dim, lax.axis_size(axis))
    arrived = lax.all_to_all(parts, axis, split_axis=0, concat_axis=0, tiled=True)
    return arrived.astype(jnp.float32).sum(axis=0)


def attend_block(
    partial_state, long_queries, key_block, value_block, key_pos, query_pos, score_scale
):
    running_max, weight_sum, weighted = partial_state
    scores = (
        jnp.einsum("qgjd,kgd->qgjk", long_queries, key_block, preferred_element_type=jnp.float32)
        * score_scale
    )
    visible = (key_pos[None, :] <= query_pos[:, None])[:, None, None, :]
    masked = jnp.where(visible, scores, -1e30)
    newest = jnp.maximum(running_max, jnp.max(masked, axis=-1))
    weights = jnp.where(visible, jnp.exp(masked - newest[..., None]), 0.0)
    factor = jnp.exp(running_max - newest)
    weight_sum = weight_sum * factor + jnp.sum(weights, axis=-1)
    weighted = weighted * factor[..., None] + jnp.einsum(
        "qgjk,kgd->qgjd",
        weights.astype(jnp.bfloat16),
        value_block,
        preferred_element_type=jnp.float32,
    )
    return (newest, weight_sum, weighted)


def rounded_term(attended, out_weight):
    product = jnp.dot(attended, out_weight, preferred_element_type=jnp.float32)
    return lax.optimization_barrier(product.astype(jnp.bfloat16)).astype(jnp.float32)


def on_device(
    queries, key_rows, value_rows, residual, out_weight, norm_gain, span_map, segments, row_owner
):
    wide_count = lax.axis_size("wide")
    narrow_count = lax.axis_size("narrow")
    wide_index = lax.axis_index("wide")
    local_heads = queries.shape[1] // HEAD
    local_kv = key_rows.shape[1] // HEAD
    group_size = local_heads // local_kv
    token_count = queries.shape[0]
    short_count = token_count - LONG_DEV
    score_scale = HEAD ** (-0.5)
    own_span = lax.dynamic_slice_in_dim(span_map, wide_index, 1, 0)[0]
    query_pos = own_span * LONG_DEV + jnp.arange(LONG_DEV, dtype=jnp.int32)
    long_queries = queries[:LONG_DEV].reshape(LONG_DEV, local_kv, group_size, HEAD)
    wide_ids = jnp.arange(wide_count, dtype=jnp.int32)
    start_state = (
        jnp.full((LONG_DEV, local_kv, group_size), -1e30, jnp.float32),
        jnp.zeros((LONG_DEV, local_kv, group_size), jnp.float32),
        jnp.zeros((LONG_DEV, local_kv, group_size, HEAD), jnp.float32),
    )
    key_piece, value_piece = sent_together(
        (key_rows[:LONG_DEV], value_rows[:LONG_DEV]), "wide", 0, 1
    )
    row_count = key_piece.shape[0]
    key_index = jnp.arange(row_count, dtype=jnp.int32)
    holder = key_index // LONG_DEV
    span_of = jnp.sum(jnp.where(holder[:, None] == wide_ids[None, :], span_map[None, :], 0), axis=1)
    key_pos = span_of * LONG_DEV + key_index % LONG_DEV
    key_block = key_piece.reshape(row_count, local_kv, HEAD)
    value_block = value_piece.reshape(row_count, local_kv, HEAD)
    splits = row_count // 512

    def advance_block(inner_state, sliced):
        return (
            attend_block(
                inner_state, long_queries, sliced[0], sliced[1], sliced[2], query_pos, score_scale
            ),
            None,
        )

    finished, unused = lax.scan(
        advance_block,
        start_state,
        (
            key_block.reshape(splits, 512, local_kv, HEAD),
            value_block.reshape(splits, 512, local_kv, HEAD),
            key_pos.reshape(splits, 512),
        ),
    )
    running_max, weight_sum, weighted = finished
    long_out = (
        (weighted / weight_sum[..., None])
        .astype(jnp.bfloat16)
        .reshape(LONG_DEV, local_heads * HEAD)
    )
    short_queries = queries[LONG_DEV:].reshape(short_count, local_kv, group_size, HEAD)
    short_keys = key_rows[LONG_DEV:].reshape(short_count, local_kv, HEAD)
    short_values = value_rows[LONG_DEV:].reshape(short_count, local_kv, HEAD)
    documents = segments[0]
    positions = jnp.arange(short_count, dtype=jnp.int32)
    visible = (
        (documents[None, :] == documents[:, None]) & (positions[None, :] <= positions[:, None])
    )[:, None, None, :]
    scores = (
        jnp.einsum("qgjd,kgd->qgjk", short_queries, short_keys, preferred_element_type=jnp.float32)
        * score_scale
    )
    masked = jnp.where(visible, scores, -1e30)
    row_max = jnp.max(masked, axis=-1, keepdims=True)
    weights = jnp.where(visible, jnp.exp(masked - row_max), 0.0)
    short_sum = jnp.sum(weights, axis=-1)
    mixed = jnp.einsum(
        "qgjk,kgd->qgjd",
        weights.astype(jnp.bfloat16),
        short_values,
        preferred_element_type=jnp.float32,
    )
    short_out = (
        (mixed / short_sum[..., None]).astype(jnp.bfloat16).reshape(short_count, local_heads * HEAD)
    )
    attended = jnp.concatenate([long_out, short_out], axis=0)
    rows_dev = token_count // narrow_count
    sliced = attended
    summed = sum_at_owner(rounded_term(sliced, out_weight).astype(jnp.bfloat16), "narrow", 0)
    hidden = (residual.astype(jnp.float32) + summed).astype(jnp.bfloat16)
    widened = hidden.astype(jnp.float32)
    normed = (
        widened
        * lax.rsqrt(jnp.mean(widened * widened, axis=1, keepdims=True) + 1e-05)
        * norm_gain.astype(jnp.float32)
    ).astype(jnp.bfloat16)
    capacity = max(2, 2 * rows_dev // wide_count)
    owners = row_owner[:, 0]
    chosen = (owners[:, None] == wide_ids[None, :]).astype(jnp.int32)
    earlier = jnp.cumsum(chosen, axis=0) - chosen
    slot_index = jnp.sum(earlier * chosen, axis=1)
    target = owners * capacity + slot_index
    dispatch = (
        target[None, :] == jnp.arange(wide_count * capacity, dtype=jnp.int32)[:, None]
    ).astype(jnp.bfloat16)
    outgoing = jnp.dot(dispatch, normed, preferred_element_type=jnp.float32).astype(jnp.bfloat16)
    outgoing = outgoing.reshape(wide_count, 1, 1, capacity, normed.shape[1])
    arrived = lax.all_to_all(outgoing, "wide", split_axis=0, concat_axis=2, tiled=True)
    return (hidden, arrived)


def solution(mesh):
    placed = (
        P(("rep", "wide"), "narrow"),
        P(("rep", "wide"), "narrow"),
        P(("rep", "wide"), "narrow"),
        P(("rep", "wide", "narrow"), None),
        P("narrow", None),
        P(),
        P(),
        P(("rep", "wide"), None),
        P(("rep", "wide", "narrow"), None),
    )
    return jax.shard_map(
        on_device,
        mesh=mesh,
        in_specs=placed,
        out_specs=(
            P(("rep", "wide", "narrow"), None),
            P(("rep", "wide"), "narrow", None, None, None),
        ),
        check_vma=False,
    )
```

profile of v0, /device:TPU:32, one launch (start us, length us, event | category | flops | bytes accessed | tf_op | source)
XLA Modules:
  0.0 234.3 jit_solution(13354712695801570120)
XLA Ops:
  9.4 1.2 dynamic_slice.14
  15.8 99.2 %all-gather.2.cloned.1.call-done = bf16[8192,256]{1,0:T(8,128)(2,1)} async-done(((bf16[128,256]{1,0:T(8,128)(2,1)}), bf16[8192,256]{1,0:T(8,128)(2,1)}) %all-gather.2.cloned.1.call-update) | async-done | bytes 4194320 | tf_op jit(solution)/shard_map/all_gather | solution.py:16
  115.0 3.8 %fusion.56 = (bf16[8192,128]{1,0:T(8,128)(2,1)S(1)}, bf16[8192,128]{1,0:T(8,128)(2,1)}) fusion(bf16[8192,256]{1,0:T(8,128)(2,1)} %all-gather.2.cloned.1.call-done), kind=kLoop, calls=%fused_computation.90 | loop fusion | bytes 8388608 | tf_op jit(solution)/shard_map/split | solution.py:16
  118.8 32.7 %while.15 = (s32[]{:T(128)}, f32[128,1,4]{0,2,1:T(4,128)S(1)}, f32[128,1,4]{0,2,1:T(4,128)S(1)}, f32[128,1,4,128]{0,3,2,1:T(8,128)S(1)}, s32[16,512]{1,0:T(8,128...) while((s32[]{:T(128)}, f32[128,1,4]{0,2,1:T(4,128)S(1)}, ...), condition=%wide.region_4.5_spmd.clone, body=%wide.region_1.4_spmd.clone.sunk | while | flops 136842368 | bytes 4365457 | solution.py:100
  119.0 1.2 fusion.69
  121.0 1.2 fusion.69
  123.1 1.2 fusion.69
  125.1 1.2 fusion.69
  127.2 1.2 fusion.69
  129.2 1.2 fusion.69
  131.3 1.2 fusion.69
  133.3 1.2 fusion.69
  135.4 1.2 fusion.69
  137.4 1.2 fusion.69
  139.4 1.2 fusion.69
  141.5 1.2 fusion.69
  143.5 1.2 fusion.69
  145.6 1.2 fusion.69
  147.6 1.2 fusion.69
  149.7 1.2 fusion.69
  151.6 4.8 %convolution_convert_fusion = bf16[256,4096]{1,0:T(8,128)(2,1)} fusion(bf16[512,4096]{1,0:T(8,128)(2,1)} %param.15, bf16[128,512]{0,1:T(8,128)(2,1)S(1)} %bitcast.116, bf16[128,512]{0,1:T(8,128)(2,1)S(1)} %bitcast.112), kind=kOutput, calls=%fused_computation.30 | convolution fusion | flops 1075314688 | bytes 6553600 | tf_op jit(solution)/shard_map/dot_general | solution.py:55
  156.4 3.7 %all-to-all-start = ((bf16[4,64,4096]{2,1,0:T(8,128)(2,1)}), bf16[4,64,4096]{2,1,0:T(8,128)(2,1)S(1)}, u32[]{:S(2)}, u32[]{:S(2)}) async-start(bf16[4,64,4096]{2,1,0:T(8,128)(2,1)} %bitcast.18), calls=%async_computation | async-start | bytes 4194304 | tf_op jit(solution)/shard_map/all_to_all | solution.py:27
  160.6 25.2 %all-to-all-done = bf16[4,64,4096]{2,1,0:T(8,128)(2,1)S(1)} async-done(((bf16[4,64,4096]{2,1,0:T(8,128)(2,1)}), bf16[4,64,4096]{2,1,0:T(8,128)(2,1)S(1)}, u32[]{:S(2)}, u32[]{:S(2)}) %all-to-all-start) | async-done | bytes 2097184 | tf_op jit(solution)/shard_map/all_to_all | solution.py:27
  187.6 38.8 %all_to_all.17 = bf16[64,1,1,2,4096]{4,3,2,1,0:T(2,128)(2,1)S(1)} all-to-all(bf16[64,1,1,2,4096]{4,3,2,1,0:T(2,128)(2,1)S(1)} %bitcast.106), channel_id=1, replica_groups=mesh['wide'=64,'narrow'=4,'rep'=4] {'wide'}, dimensions={0} | all-to-all | bytes 2097152 | tf_op jit(solution)/shard_map/all_to_all | solution.py:162
  (171 shorter events, 22.0 us)
Async XLA Ops:
  7.2 8.5 %copy-start.2 = (bf16[256,128]{1,0:T(8,128)(2,1)S(1)}, bf16[256,128]{1,0:T(8,128)(2,1)}, u32[]{:S(2)}) copy-start(bf16[256,128]{1,0:T(8,128)(2,1)} %param.13) | copy-start | bytes 196612
  7.2 107.8 %all-gather.2.cloned.1.call-start = ((), (), s32[]{:S(2)}) async-start(), calls=%async_computation.2 | async-start | bytes 4259840 | tf_op jit(solution)/shard_map/all_gather | solution.py:16
  156.4 3.8 %copy-start.3 = (bf16[4096]{0:T(1024)(128)(2,1)S(1)}, bf16[4096]{0:T(1024)(128)(2,1)}, u32[]{:S(2)}) copy-start(bf16[4096]{0:T(1024)(128)(2,1)} %param.16) | copy-start | bytes 24580
  156.4 3.8 %copy-start.4 = (s32[64,1]{0,1:T(1,128)S(1)}, s32[64,1]{0,1:T(1,128)}, u32[]{:S(2)}) copy-start(s32[64,1]{0,1:T(1,128)} %param.19) | copy-start | bytes 772
  156.4 29.4 %all-to-all-start = ((bf16[4,64,4096]{2,1,0:T(8,128)(2,1)}), bf16[4,64,4096]{2,1,0:T(8,128)(2,1)S(1)}, u32[]{:S(2)}, u32[]{:S(2)}) async-start(bf16[4,64,4096]{2,1,0:T(8,128)(2,1)} %bitcast.18), calls=%async_computation | async-start | bytes 4194304 | tf_op jit(solution)/shard_map/all_to_all | solution.py:27
  160.2 25.9 %copy-start.1 = (bf16[64,4096]{1,0:T(8,128)(2,1)S(1)}, bf16[64,4096]{1,0:T(8,128)(2,1)}, u32[]{:S(2)}) copy-start(bf16[64,4096]{1,0:T(8,128)(2,1)} %param.14) | copy-start | bytes 1572868
  186.4 40.1 %copy-start = (bf16[64,4096]{1,0:T(8,128)(2,1)}, bf16[64,4096]{1,0:T(8,128)(2,1)S(1)}, u32[]{:S(2)}) copy-start(bf16[64,4096]{1,0:T(8,128)(2,1)S(1)} %get-tuple-element.240) | copy-start | bytes 1572868
Sparse Core Ops, SparseCore 0:
  12.8 102.1 all-gather.1
where the time goes:
time: 235 us; the launch traced here: 234 us
  waiting for transfers between devices  124 us (53%)
  blocking collectives  38.8 us (17%)
  matrix products  31.9 us (14%)
  between operations  14.8 us (6%)
  local copies, waits for them, and re-layouts  9.91 us (4%)
  other arithmetic  9.59 us (4%)
  starting transfers between devices  3.78 us (2%)
    all_gather x1, waiting for transfers between devices, sent_together(): lax.all_gather(both, axis, axis=dim, tiled=True)  99.2 us
    all_to_all x1, blocking collectives, on_device(): lax.all_to_all(outgoing, 'wide', split_axis=0, concat_axis=2, tiled=True)  38.8 us
    all_to_all x1, waiting for transfers between devices, sum_at_owner(): lax.all_to_all(parts, axis, split_axis=0, concat_axis=0, tiled=True)  25.2 us
    dot_general x16, matrix products, attend_block(): jnp.einsum('qgjd,kgd->qgjk', long_queries, key_block, preferred_element_t...  19.5 us
    dot_general x16, matrix products, attend_block(): jnp.einsum('qgjk,kgd->qgjd', weights.astype(jnp.bfloat16), value_block, p...  5.89 us
    dot_general x1, matrix products, rounded_term(): product = jnp.dot(attended, out_weight, preferred_element_type=jnp.float32)  4.82 us
  transfers between devices with their start and end apart: 2, of which 2 were waited for; matrix products, arithmetic and copies ran while one was open for 3% of the time, Pallas kernels for 0%

commit v1 on v0

v1 whole, which is shorter than its diff:
```python
import jax
import jax.numpy as jnp
from jax import lax
from jax.experimental import pallas as pl
from jax.experimental.pallas import tpu as pltpu
from jax.sharding import PartitionSpec as P

HEAD = 128
LONG_DEV = 128
SIDE = 8
HEADS = 4
SCALE = HEAD ** (-0.5)
FAR = -1e30
STATS = 16
QUERY_GROUPS = [
    [(2 * b + j) * SIDE + 2 * a + i for j in range(2) for i in range(2)]
    for b in range(4)
    for a in range(4)
]
KEY_GROUPS = [
    [(2 * b + j) * SIDE + 2 * a + i for b in range(4) for a in range(4)]
    for j in range(2)
    for i in range(2)
]


def dot_nt(a, b):
    return lax.dot_general(a, b, (((1,), (1,)), ((), ())), preferred_element_type=jnp.float32)


def dot_tn(a, b):
    return lax.dot_general(a, b, (((0,), (0,)), ((), ())), preferred_element_type=jnp.float32)


def heads_down(q):
    return jnp.concatenate([q[:, h * HEAD : (h + 1) * HEAD] for h in range(HEADS)], axis=0)


def heads_across(o):
    return jnp.concatenate(
        [o[:, h * HEAD : (h + 1) * HEAD].T for h in range(HEADS)], axis=1
    )


def prep_kernel(q_ref, k_ref, v_ref, seg_ref, kv_out, q_out, short_out):
    kv = jnp.concatenate([k_ref[:LONG_DEV], v_ref[:LONG_DEV]], axis=1)
    for i in range(kv_out.shape[0]):
        kv_out[i] = kv
    q = q_ref[:LONG_DEV]
    for j in range(q_out.shape[0]):
        q_out[j] = q
    qs = heads_down(q_ref[LONG_DEV:])
    k = k_ref[LONG_DEV:]
    v = v_ref[LONG_DEV:]
    n = k.shape[0]
    seg_q = jnp.broadcast_to(seg_ref[...].astype(jnp.float32), (n, n))
    seg_k = seg_q.T
    row = lax.broadcasted_iota(jnp.int32, (n, n), 0)
    col = lax.broadcasted_iota(jnp.int32, (n, n), 1)
    visible = jnp.where((seg_q == seg_k) & (row <= col), 1.0, 0.0)
    visible = jnp.concatenate([visible] * HEADS, axis=1) > 0.5
    s = dot_nt(k, qs) * SCALE
    s = jnp.where(visible, s, FAR)
    top = jnp.max(s, axis=0, keepdims=True)
    w = jnp.where(visible, jnp.exp(s - top), 0.0)
    total = jnp.sum(w, axis=0, keepdims=True)
    o = dot_tn(v, w.astype(jnp.bfloat16)) / total
    short_out[...] = heads_across(o).astype(jnp.bfloat16)


def three_parts(x):
    high = x.astype(jnp.bfloat16).astype(jnp.float32)
    rest = x - high
    middle = rest.astype(jnp.bfloat16).astype(jnp.float32)
    return high, middle, rest - middle


def attend_kernel(wide_ref, span_ref, q_ref, kv_ref, out_ref, top_ref, sum_ref, acc_ref):
    j = pl.program_id(0)
    w = wide_ref[0]
    y = w // SIDE
    x = w % SIDE
    q_span = span_ref[((y // 2) * 2 + j // 2) * SIDE + (x // 2) * 2 + j % 2]
    qs = heads_down(q_ref[0])
    cols = qs.shape[0]
    top_ref[...] = jnp.full(top_ref.shape, FAR, jnp.float32)
    sum_ref[...] = jnp.zeros(sum_ref.shape, jnp.float32)
    acc_ref[...] = jnp.zeros(acc_ref.shape, jnp.float32)
    step = 2
    rows = step * LONG_DEV

    def advance(c, visible):
        k = kv_ref[c * step : (c + 1) * step, :, :HEAD].reshape(rows, HEAD)
        v = kv_ref[c * step : (c + 1) * step, :, HEAD:].reshape(rows, HEAD)
        s = dot_nt(k, qs)
        if visible is not None:
            s = jnp.where(visible, s, FAR)
        old = top_ref[...]
        new = jnp.maximum(old, jnp.max(s, axis=0, keepdims=True))
        p = jnp.exp((s - new) * SCALE)
        if visible is not None:
            p = jnp.where(visible, p, 0.0)
        factor = jnp.exp((old - new) * SCALE)
        top_ref[...] = new
        sum_ref[...] = sum_ref[...] * factor + jnp.sum(p, axis=0, keepdims=True)
        acc_ref[...] = acc_ref[...] * factor + dot_tn(v, p.astype(jnp.bfloat16))

    for c in range(kv_ref.shape[0] // step):
        spans = []
        for i in range(c * step, (c + 1) * step):
            spans.append(span_ref[((i // 4) * 2 + y % 2) * SIDE + (i % 4) * 2 + x % 2])
        low = jnp.minimum(spans[0], spans[1])
        high = jnp.maximum(spans[0], spans[1])

        @pl.when(high < q_span)
        def _(c=c):
            advance(c, None)

        @pl.when((low <= q_span) & (high >= q_span))
        def _(c=c, spans=spans):
            row = lax.broadcasted_iota(jnp.int32, (rows, cols), 0)
            col = lax.broadcasted_iota(jnp.int32, (rows, cols), 1)
            place = row % LONG_DEV
            key_pos = jnp.where(row < LONG_DEV, spans[0], spans[1]) * LONG_DEV + place
            query_pos = q_span * LONG_DEV + col % LONG_DEV
            advance(c, key_pos <= query_pos)

    total = sum_ref[...]
    o = acc_ref[...] / jnp.where(total > 0.0, total, 1.0)
    out_ref[0, :HEAD] = o.astype(jnp.bfloat16)
    parts = (*three_parts(top_ref[...] * SCALE), *three_parts(total))
    row = lax.broadcasted_iota(jnp.int32, (STATS, cols), 0)
    stats = jnp.zeros((STATS, cols), jnp.float32)
    for i, part in enumerate(parts):
        stats = jnp.where(row == i, part, stats)
    out_ref[0, HEAD:] = stats.astype(jnp.bfloat16)


def project_kernel(core_ref, got_ref, short_ref, weight_ref, send_ref, keep_ref, rows_ref):
    half = LONG_DEV // 2

    @pl.when(pl.program_id(0) == 0)
    def _():
        core = core_ref[0]
        tops, sums = [], []
        for j in range(got_ref.shape[0]):
            stats = got_ref[j, HEAD:].astype(jnp.float32)
            tops.append(stats[0:1] + stats[1:2] + stats[2:3])
            sums.append(stats[3:4] + stats[4:5] + stats[5:6])
        top = jnp.maximum(jnp.maximum(tops[0], tops[1]), jnp.maximum(tops[2], tops[3]))
        shares = [s * jnp.exp(t - top) for s, t in zip(sums, tops)]
        total = (shares[0] + shares[1]) + (shares[2] + shares[3])
        o = got_ref[0, :HEAD].astype(jnp.float32) * (shares[0] / total)
        for j in range(1, 4):
            o = o + got_ref[j, :HEAD].astype(jnp.float32) * (shares[j] / total)
        long = heads_across(o).astype(jnp.bfloat16)
        short = short_ref[...]
        for b in range(2):
            at = pl.multiple_of(jnp.where(core == b, 2 * half, 0), half)
            rows_ref[pl.ds(at, half), :] = long[b * half : (b + 1) * half]
            rows_ref[pl.ds(at + half, half), :] = short[b * half : (b + 1) * half]

    product = jnp.dot(rows_ref[...], weight_ref[...], preferred_element_type=jnp.float32)
    rounded = product.astype(jnp.bfloat16)
    send_ref[...] = rounded[: 2 * half]
    keep_ref[...] = rounded[2 * half :]


def pair_kernel(row_ref, keep_ref, got_ref, out_ref):
    out_ref[...] = (
        keep_ref[...].astype(jnp.float32) + got_ref[...].astype(jnp.float32)
    ).astype(jnp.bfloat16)


def route_kernel(
    row_ref, res_ref, keep_ref, got_ref, far_ref, gain_ref, owner_ref, hidden_ref, out_ref, wide_ref
):
    summed = (keep_ref[...].astype(jnp.float32) + got_ref[...].astype(jnp.float32)) + far_ref[
        ...
    ].astype(jnp.float32)
    hidden = (res_ref[...].astype(jnp.float32) + summed).astype(jnp.bfloat16)
    hidden_ref[...] = hidden
    h = hidden.astype(jnp.float32)
    mean = jnp.mean(h * h, axis=1, keepdims=True)
    normed = (h * lax.rsqrt(mean + 1e-05) * gain_ref[...].astype(jnp.float32)).astype(jnp.bfloat16)
    rows = h.shape[0]
    down = jnp.broadcast_to(owner_ref[...].astype(jnp.float32), (rows, HEAD))
    across = down.T[:rows]
    row = lax.broadcasted_iota(jnp.int32, (rows, rows), 0)
    col = lax.broadcasted_iota(jnp.int32, (rows, rows), 1)
    same = (down[:, :rows] == across) & (row < col)
    slot = jnp.sum(jnp.where(same, 1.0, 0.0), axis=0, keepdims=True)
    mine = across == row.astype(jnp.float32)
    owners = rows
    stride = out_ref.shape[0] // owners
    for s in range(2):
        pick = jnp.where(mine & (slot == float(s)), 1.0, 0.0).astype(jnp.bfloat16)
        placed = jnp.dot(pick, normed, preferred_element_type=jnp.float32)
        for t in range(stride // 2):
            wide_ref[pl.ds(2 * t + s, owners, stride=stride), :] = placed[
                :, t * HEAD : (t + 1) * HEAD
            ]
    out_ref[...] = wide_ref[...].astype(jnp.bfloat16)


def exchange(x, groups=None):
    return lax.all_to_all(x, "wide", 0, 0, tiled=True, axis_index_groups=groups)


def on_device(
    queries, key_rows, value_rows, residual, out_weight, norm_gain, span_map, segments, row_owner
):
    wide = lax.axis_index("wide").astype(jnp.int32).reshape(1)
    narrow = lax.axis_index("narrow").astype(jnp.int32).reshape(1)
    core = narrow & 1
    level = lax.shift_right_logical(narrow, jnp.ones_like(narrow))
    bf = jnp.bfloat16
    cols = queries.shape[1]
    width = out_weight.shape[1]
    kv, qs, short = pl.pallas_call(
        prep_kernel,
        out_shape=(
            jax.ShapeDtypeStruct((16, LONG_DEV, 2 * HEAD), bf),
            jax.ShapeDtypeStruct((4, LONG_DEV, cols), bf),
            jax.ShapeDtypeStruct((LONG_DEV, cols), bf),
        ),
        name="prep",
    )(queries, key_rows, value_rows, segments)
    qs = exchange(qs, QUERY_GROUPS)
    kv = exchange(kv, KEY_GROUPS)
    parts = pl.pallas_call(
        attend_kernel,
        grid_spec=pltpu.PrefetchScalarGridSpec(
            num_scalar_prefetch=2,
            grid=(4,),
            in_specs=[
                pl.BlockSpec((1, LONG_DEV, cols), lambda j, w, m: (j, 0, 0)),
                pl.BlockSpec((16, LONG_DEV, 2 * HEAD), lambda j, w, m: (0, 0, 0)),
            ],
            out_specs=pl.BlockSpec((1, HEAD + STATS, cols), lambda j, w, m: (j, 0, 0)),
            scratch_shapes=[
                pltpu.VMEM((1, cols), jnp.float32),
                pltpu.VMEM((1, cols), jnp.float32),
                pltpu.VMEM((HEAD, cols), jnp.float32),
            ],
        ),
        out_shape=jax.ShapeDtypeStruct((4, HEAD + STATS, cols), bf),
        name="attend",
    )(wide, span_map, qs, kv)
    got = exchange(parts, QUERY_GROUPS)
    block = 1024
    send, keep = pl.pallas_call(
        project_kernel,
        grid_spec=pltpu.PrefetchScalarGridSpec(
            num_scalar_prefetch=1,
            grid=(width // block,),
            in_specs=[
                pl.BlockSpec((4, HEAD + STATS, cols), lambda i, c: (0, 0, 0)),
                pl.BlockSpec((LONG_DEV, cols), lambda i, c: (0, 0)),
                pl.BlockSpec((cols, block), lambda i, c: (0, i)),
            ],
            out_specs=[
                pl.BlockSpec((LONG_DEV, block), lambda i, c: (0, i)),
                pl.BlockSpec((LONG_DEV, block), lambda i, c: (0, i)),
            ],
            scratch_shapes=[pltpu.VMEM((2 * LONG_DEV, cols), bf)],
        ),
        out_shape=(
            jax.ShapeDtypeStruct((LONG_DEV, width), bf),
            jax.ShapeDtypeStruct((LONG_DEV, width), bf),
        ),
        name="project",
    )(core, got, short, out_weight)
    near = lax.ppermute(send, "narrow", [(0, 1), (1, 0), (2, 3), (3, 2)])
    rows = residual.shape[0]
    mine = pl.BlockSpec((rows, width), lambda i, r: (r[0], 0))
    whole = pl.BlockSpec((rows, width), lambda i, r: (0, 0))
    pair = pl.pallas_call(
        pair_kernel,
        grid_spec=pltpu.PrefetchScalarGridSpec(
            num_scalar_prefetch=1, grid=(1,), in_specs=[mine, mine], out_specs=whole
        ),
        out_shape=jax.ShapeDtypeStruct((rows, width), bf),
        name="pair",
    )(1 - level, keep, near)
    far = lax.ppermute(pair, "narrow", [(0, 2), (2, 0), (1, 3), (3, 1)])
    owners = 64
    tiles = 2 * width // HEAD
    hidden, outgoing = pl.pallas_call(
        route_kernel,
        grid_spec=pltpu.PrefetchScalarGridSpec(
            num_scalar_prefetch=1,
            grid=(1,),
            in_specs=[
                whole,
                mine,
                mine,
                whole,
                pl.BlockSpec((1, width), lambda i, r: (0, 0)),
                pl.BlockSpec((rows, 1), lambda i, r: (0, 0)),
            ],
            out_specs=[whole, pl.BlockSpec((owners * tiles, HEAD), lambda i, r: (0, 0))],
            scratch_shapes=[pltpu.VMEM((owners * tiles, HEAD), jnp.float32)],
        ),
        out_shape=(
            jax.ShapeDtypeStruct((rows, width), bf),
            jax.ShapeDtypeStruct((owners * tiles, HEAD), bf),
        ),
        name="route",
    )(level, residual, keep, near, far, norm_gain.reshape(1, width), row_owner)
    arrived = exchange(outgoing.reshape(owners, tiles, HEAD))
    arrived = arrived.reshape(owners, tiles // 2, 2, HEAD).transpose(0, 2, 1, 3)
    return (hidden, arrived.reshape(1, 1, owners, 2, width))


def solution(mesh):
    placed = (
        P(("rep", "wide"), "narrow"),
        P(("rep", "wide"), "narrow"),
        P(("rep", "wide"), "narrow"),
        P(("rep", "wide", "narrow"), None),
        P("narrow", None),
        P(),
        P(),
        P(("rep", "wide"), None),
        P(("rep", "wide", "narrow"), None),
    )
    return jax.shard_map(
        on_device,
        mesh=mesh,
        in_specs=placed,
        out_specs=(
            P(("rep", "wide", "narrow"), None),
            P(("rep", "wide"), "narrow", None, None, None),
        ),
        check_vma=False,
    )
```

time: 235 us -> 166 us (0.71)
  the two profiles are of different devices: /device:TPU:32 before, /device:TPU:288 now
where the time goes in v1:
time: 166 us; the launch traced here: 167 us
  blocking collectives  59.4 us (36%)
  waiting for transfers between devices  50 us (30%)
  Pallas kernels  26.5 us (16%)
  starting transfers between devices  23.6 us (14%)
  local copies, waits for them, and re-layouts  6.27 us (4%)
    all_to_all x2, blocking collectives, exchange(): return lax.all_to_all(x, 'wide', 0, 0, tiled=True, axis_index_groups=groups)  59.4 us
    all_to_all x2, waiting for transfers between devices, exchange(): return lax.all_to_all(x, 'wide', 0, 0, tiled=True, axis_index_groups=groups)  36.1 us
    all_to_all x2, starting transfers between devices, exchange(): return lax.all_to_all(x, 'wide', 0, 0, tiled=True, axis_index_groups=groups)  16.5 us
    pallas_call x1, Pallas kernels, on_device(): pl.pallas_call(attend_kernel, grid_spec=pltpu.PrefetchScalarGridSpec(num_...  12 us
    ppermute x1, waiting for transfers between devices, on_device(): far = lax.ppermute(pair, 'narrow', [(0, 2), (2, 0), (1, 3), (3, 1)])  11.1 us
    pallas_call x1, Pallas kernels, on_device(): pl.pallas_call(project_kernel, grid_spec=pltpu.PrefetchScalarGridSpec(num...  5.35 us
    ppermute x1, starting transfers between devices, on_device(): far = lax.ppermute(pair, 'narrow', [(0, 2), (2, 0), (1, 3), (3, 1)])  5.23 us
    pallas_call x1, Pallas kernels, on_device(): pl.pallas_call(route_kernel, grid_spec=pltpu.PrefetchScalarGridSpec(num_s...  4.5 us
  transfers between devices with their start and end apart: 4, of which 4 were waited for; matrix products, arithmetic and copies ran while one was open for 1% of the time, Pallas kernels for 0%

profile of v1, /device:TPU:288, one launch (start us, length us, event | category | flops | bytes accessed | tf_op | source)
XLA Modules:
  0.0 166.5 jit_solution(391141154694761244)
XLA Ops:
  0.6 2.6 %prep.1 = (bf16[16,128,256]{2,1,0:T(8,128)(2,1)}, bf16[4,128,512]{2,1,0:T(8,128)(2,1)}, bf16[128,512]{1,0:T(8,128)(2,1)}) custom-call(bf16[256,512]{1,0:T(8,128)(2,1)} %q_ref.1, bf16[256,128]{1,0:T(8,128)(2,1)} %k_ref.1, bf16[256,128]{1,0:T(8,128)(2,1)} %v_ref.1, s32[1,128]{1,0:T(1,128)} %seg_ref.1), custom_call_target="tpu_custom_call" | custom-call | tf_op jit(solution)/shard_map/prep/pallas_call | solution.py:220
  3.2 13.0 %all_to_all.20.q_ref = bf16[4,128,512]{2,1,0:T(8,128)(2,1)} all-to-all(bf16[4,128,512]{2,1,0:T(8,128)(2,1)} %get-tuple-element.9), channel_id=1, replica_groups={{0,16,128,144},{32,48,160,176},{64,80,192,208},{96,112,224,240},{256,27..., dimensions={0} | all-to-all | bytes 1048576 | tf_op jit(solution)/shard_map/all_to_all | solution.py:207
  16.2 12.6 %all-to-all-start.1 = ((bf16[16,128,256]{2,1,0:T(8,128)(2,1)}), bf16[16,128,256]{2,1,0:T(8,128)(2,1)S(1)}, u32[]{:S(2)}, u32[]{:S(2)}) async-start(bf16[16,128,256]{2,1,0:T(8,128)(2,1)} %get-tuple-element.10), calls=%async_computation.1 | async-start | bytes 2097152 | tf_op jit(solution)/shard_map/all_to_all | solution.py:207
  28.8 27.1 %all-to-all-done.1.kv_ref = bf16[16,128,256]{2,1,0:T(8,128)(2,1)S(1)} async-done(((bf16[16,128,256]{2,1,0:T(8,128)(2,1)}), bf16[16,128,256]{2,1,0:T(8,128)(2,1)S(1)}, u32[]{:S(2)}, u32[]{:S(2)}) %all-to-all-start.1) | async-done | bytes 1048608 | tf_op jit(solution)/shard_map/all_to_all | solution.py:207
  55.9 1.0 copy-done.1
  56.9 12.0 %attend.1 = bf16[4,144,512]{2,1,0:T(8,128)(2,1)} custom-call(s32[1]{0:T(128)} %bitcast.2.wide_ref, s32[64]{0:T(128)} %span_ref.1, bf16[4,128,512]{2,1,0:T(8,128)(2,1)} %all_to_all.20.q_ref, bf16[16,128,256]{2,1,0:T(8,128)(2,1)} %copy-done.1), custom_call_target="tpu_custom_call" | custom-call | tf_op jit(solution)/shard_map/attend/pallas_call | solution.py:231
  68.9 3.9 %all-to-all-start.2 = ((bf16[4,144,512]{2,1,0:T(8,128)(2,1)}), bf16[4,144,512]{2,1,0:T(8,128)(2,1)S(1)}, u32[]{:S(2)}, u32[]{:S(2)}) async-start(bf16[4,144,512]{2,1,0:T(8,128)(2,1)} %attend.1), calls=%async_computation.2 | async-start | bytes 1179648 | tf_op jit(solution)/shard_map/all_to_all | solution.py:207
  72.7 9.1 %all-to-all-done.2.got_ref = bf16[4,144,512]{2,1,0:T(8,128)(2,1)S(1)} async-done(((bf16[4,144,512]{2,1,0:T(8,128)(2,1)}), bf16[4,144,512]{2,1,0:T(8,128)(2,1)S(1)}, u32[]{:S(2)}, u32[]{:S(2)}) %all-to-all-start.2) | async-done | bytes 589856 | tf_op jit(solution)/shard_map/all_to_all | solution.py:207
  81.8 0.9 copy-done.2
  82.6 5.3 %project.1 = (bf16[128,4096]{1,0:T(8,128)(2,1)}, bf16[128,4096]{1,0:T(8,128)(2,1)}) custom-call(s32[1]{0:T(128)} %bitcast.1.core_ref, bf16[4,144,512]{2,1,0:T(8,128)(2,1)} %copy-done.2, bf16[128,512]{1,0:T(8,128)(2,1)} %get-tuple-element.11.short_ref, bf16[512,4096]{1,0:T(8,128)(2,1)} %weight_ref.1), custom_call_target="tpu_custom_call" | custom-call | tf_op jit(solution)/shard_map/project/pallas_call | solution.py:252
  88.0 1.9 %collective-permute-start = (bf16[128,4096]{1,0:T(8,128)(2,1)}, bf16[128,4096]{1,0:T(8,128)(2,1)S(1)}, u32[]{:S(2)}, u32[]{:S(2)}) collective-permute-start(bf16[128,4096]{1,0:T(8,128)(2,1)} %get-tuple-element.13), channel_id=1, source_target_pairs={{0,4},{4,0},{8,12},{12,8},{1,5},{5,1},{9,13},{13,9},{2,6},{6,2},{1... | collective-permute-start | bytes 3145736 | tf_op jit(solution)/shard_map/ppermute | solution.py:274
  89.9 2.8 %collective-permute-done.got_ref = bf16[128,4096]{1,0:T(8,128)(2,1)S(1)} collective-permute-done((bf16[128,4096]{1,0:T(8,128)(2,1)}, bf16[128,4096]{1,0:T(8,128)(2,1)S(1)}, u32[]{:S(2)}, u32[]{:S(2)}) %collective-permute-start) | collective-permute-done | bytes 1048608 | tf_op jit(solution)/shard_map/ppermute | solution.py:274
  92.7 1.0 copy-done
  93.7 2.1 %pair.1 = bf16[64,4096]{1,0:T(8,128)(2,1)} custom-call(s32[1]{0:T(128)S(6)} %sub.3.row_ref, bf16[128,4096]{1,0:T(8,128)(2,1)} %get-tuple-element.12.keep_ref, bf16[128,4096]{1,0:T(8,128)(2,1)} %copy-done), custom_call_target="tpu_custom_call" | custom-call | tf_op jit(solution)/shard_map/pair/pallas_call | solution.py:278
  95.8 5.2 %collective-permute-start.1 = (bf16[64,4096]{1,0:T(8,128)(2,1)}, bf16[64,4096]{1,0:T(8,128)(2,1)S(1)}, u32[]{:S(2)}, u32[]{:S(2)}) collective-permute-start(bf16[64,4096]{1,0:T(8,128)(2,1)} %pair.1), channel_id=1, source_target_pairs={{0,8},{8,0},{4,12},{12,4},{1,9},{9,1},{5,13},{13,5},{2,10},{10,2},... | collective-permute-start | bytes 1572872 | tf_op jit(solution)/shard_map/ppermute | solution.py:286
  101.1 0.6 reshape.25.gain_ref
  101.7 0.0 copy-done.5
  101.7 0.7 copy.11.owner_ref
  102.4 11.1 %collective-permute-done.1.far_ref = bf16[64,4096]{1,0:T(8,128)(2,1)S(1)} collective-permute-done((bf16[64,4096]{1,0:T(8,128)(2,1)}, bf16[64,4096]{1,0:T(8,128)(2,1)S(1)}, u32[]{:S(2)}, u32[]{:S(2)}) %collective-permute-start.1) | collective-permute-done | bytes 524320 | tf_op jit(solution)/shard_map/ppermute | solution.py:286
  113.5 0.8 copy-done.3
  114.3 4.5 %route.1 = (bf16[64,4096]{1,0:T(8,128)(2,1)}, bf16[4096,128]{1,0:T(8,128)(2,1)}) custom-call(s32[1]{0:T(128)} %bitcast.row_ref, bf16[64,4096]{1,0:T(8,128)(2,1)} %res_ref.1, bf16[128,4096]{1,0:T(8,128)(2,1)} %get-tuple-element.12.keep_ref, bf16[128,4096]{1,0:T(8,128)(2,1)} %copy-done, bf16[64,4096]{1,0:T(8,128)(2,1)} %copy-done.3, ...), custom_call_target="tpu_custom_call" | custom-call | tf_op jit(solution)/shard_map/route/pallas_call | solution.py:289
  118.8 46.4 %all_to_all.21 = bf16[64,64,128]{2,1,0:T(8,128)(2,1)S(1)} all-to-all(bf16[64,64,128]{2,1,0:T(8,128)(2,1)} %bitcast.12), channel_id=1, replica_groups=mesh['wide'=64,'narrow'=4,'rep'=4] {'wide'}, dimensions={0} | all-to-all | bytes 2097152 | tf_op jit(solution)/shard_map/all_to_all | solution.py:207
  165.1 0.2 copy.14
  165.4 1.1 reshape.28
  (7 shorter events, 0.0 us)
Async XLA Ops:
  16.2 39.7 %all-to-all-start.1 = ((bf16[16,128,256]{2,1,0:T(8,128)(2,1)}), bf16[16,128,256]{2,1,0:T(8,128)(2,1)S(1)}, u32[]{:S(2)}, u32[]{:S(2)}) async-start(bf16[16,128,256]{2,1,0:T(8,128)(2,1)} %get-tuple-element.10), calls=%async_computation.1 | async-start | bytes 2097152 | tf_op jit(solution)/shard_map/all_to_all | solution.py:207
  55.9 1.0 copy-start.1
  68.9 32.2 %copy-start.4 = (bf16[4096]{0:T(1024)(128)(2,1)S(1)}, bf16[4096]{0:T(1024)(128)(2,1)}, u32[]{:S(2)}) copy-start(bf16[4096]{0:T(1024)(128)(2,1)} %param.14) | copy-start | bytes 24580
  68.9 32.8 %copy-start.5 = (s32[64,1]{0,1:T(1,128)S(1)}, s32[64,1]{0,1:T(1,128)}, u32[]{:S(2)}) copy-start(s32[64,1]{0,1:T(1,128)} %param.17) | copy-start | bytes 772
  68.9 12.9 %all-to-all-start.2 = ((bf16[4,144,512]{2,1,0:T(8,128)(2,1)}), bf16[4,144,512]{2,1,0:T(8,128)(2,1)S(1)}, u32[]{:S(2)}, u32[]{:S(2)}) async-start(bf16[4,144,512]{2,1,0:T(8,128)(2,1)} %attend.1), calls=%async_computation.2 | async-start | bytes 1179648 | tf_op jit(solution)/shard_map/all_to_all | solution.py:207
  81.8 0.9 copy-start.2
  88.0 4.8 %collective-permute-start = (bf16[128,4096]{1,0:T(8,128)(2,1)}, bf16[128,4096]{1,0:T(8,128)(2,1)S(1)}, u32[]{:S(2)}, u32[]{:S(2)}) collective-permute-start(bf16[128,4096]{1,0:T(8,128)(2,1)} %get-tuple-element.13), channel_id=1, source_target_pairs={{0,4},{4,0},{8,12},{12,8},{1,5},{5,1},{9,13},{13,9},{2,6},{6,2},{1... | collective-permute-start | bytes 3145736 | tf_op jit(solution)/shard_map/ppermute | solution.py:274
  92.7 1.0 copy-start
  95.8 17.7 %collective-permute-start.1 = (bf16[64,4096]{1,0:T(8,128)(2,1)}, bf16[64,4096]{1,0:T(8,128)(2,1)S(1)}, u32[]{:S(2)}, u32[]{:S(2)}) collective-permute-start(bf16[64,4096]{1,0:T(8,128)(2,1)} %pair.1), channel_id=1, source_target_pairs={{0,8},{8,0},{4,12},{12,4},{1,9},{9,1},{5,13},{13,5},{2,10},{10,2},... | collective-permute-start | bytes 1572872 | tf_op jit(solution)/shard_map/ppermute | solution.py:286
  113.5 0.8 copy-start.3

commit v2 on v1

v2 whole, which is shorter than its diff:
```python
import jax
import jax.numpy as jnp
from jax import lax
from jax.experimental import pallas as pl
from jax.experimental.pallas import tpu as pltpu
from jax.sharding import PartitionSpec as P

HEAD = 128
LONG_DEV = 128
SIDE = 8
HEADS = 4
SCALE = HEAD ** (-0.5)
FAR = -1e30
STATS = 16
STEP = 4
SCALE2 = SCALE * 1.4426950408889634
QUERY_GROUPS = [
    [(2 * b + j) * SIDE + 2 * a + i for j in range(2) for i in range(2)]
    for b in range(4)
    for a in range(4)
]
KEY_GROUPS = [
    [(2 * b + j) * SIDE + 2 * a + i for b in range(4) for a in range(4)]
    for j in range(2)
    for i in range(2)
]


def dot_nt(a, b):
    return lax.dot_general(a, b, (((1,), (1,)), ((), ())), preferred_element_type=jnp.float32)


def dot_tn(a, b):
    return lax.dot_general(a, b, (((0,), (0,)), ((), ())), preferred_element_type=jnp.float32)


def heads_down(q):
    return jnp.concatenate([q[:, h * HEAD : (h + 1) * HEAD] for h in range(HEADS)], axis=0)


def heads_across(o):
    return jnp.concatenate(
        [o[:, h * HEAD : (h + 1) * HEAD].T for h in range(HEADS)], axis=1
    )


def prep_kernel(q_ref, k_ref, v_ref, kv_out, q_out):
    kv = jnp.concatenate([k_ref[:LONG_DEV], v_ref[:LONG_DEV]], axis=1)
    for i in range(kv_out.shape[0]):
        kv_out[i] = kv
    q = q_ref[:LONG_DEV]
    for j in range(q_out.shape[0]):
        q_out[j] = q


def short_rows(q_ref, k_ref, v_ref, seg_ref):
    qs = heads_down(q_ref[LONG_DEV:])
    k = k_ref[LONG_DEV:]
    v = v_ref[LONG_DEV:]
    n = k.shape[0]
    seg_q = jnp.broadcast_to(seg_ref[...].astype(jnp.float32), (n, n))
    seg_k = seg_q.T
    row = lax.broadcasted_iota(jnp.int32, (n, n), 0)
    col = lax.broadcasted_iota(jnp.int32, (n, n), 1)
    visible = jnp.where((seg_q == seg_k) & (row <= col), 1.0, 0.0)
    visible = jnp.concatenate([visible] * HEADS, axis=1) > 0.5
    s = dot_nt(k, qs) * SCALE
    s = jnp.where(visible, s, FAR)
    top = jnp.max(s, axis=0, keepdims=True)
    w = jnp.where(visible, jnp.exp(s - top), 0.0)
    total = jnp.sum(w, axis=0, keepdims=True)
    o = dot_tn(v, w.astype(jnp.bfloat16)) / total
    return heads_across(o).astype(jnp.bfloat16)


def three_parts(x):
    high = x.astype(jnp.bfloat16).astype(jnp.float32)
    rest = x - high
    middle = rest.astype(jnp.bfloat16).astype(jnp.float32)
    return high, middle, rest - middle


def attend_kernel(
    wide_ref, span_ref, q_ref, kv_ref, out_ref, list_ref, top_ref, sum_ref, acc_ref
):
    j = pl.program_id(0)
    w = wide_ref[0]
    y = w // SIDE
    x = w % SIDE
    q_span = span_ref[((y // 2) * 2 + j // 2) * SIDE + (x // 2) * 2 + j % 2]
    qs = heads_down(q_ref[j])
    cols = qs.shape[0]
    count = jnp.int32(0)
    for i in range(kv_ref.shape[0]):
        span = span_ref[((i // 4) * 2 + y % 2) * SIDE + (i % 4) * 2 + x % 2]
        list_ref[count] = i
        count = count + jnp.where(span < q_span, 1, 0)
    for i in range(STEP):
        list_ref[count + i] = 0
    own = j == (y % 2) * 2 + x % 2

    def block(i):
        return kv_ref[i, :, :HEAD], kv_ref[i, :, HEAD:]

    @pl.when(own)
    def _():
        k, v = block((y // 2) * 4 + x // 2)
        row = lax.broadcasted_iota(jnp.int32, (LONG_DEV, cols), 0)
        col = lax.broadcasted_iota(jnp.int32, (LONG_DEV, cols), 1)
        s = jnp.where(row <= col % LONG_DEV, dot_nt(k, qs), FAR)
        top = jnp.max(s, axis=0, keepdims=True)
        p = jnp.exp2((s - top) * SCALE2)
        top_ref[...] = top
        sum_ref[...] = jnp.sum(p, axis=0, keepdims=True)
        acc_ref[...] = dot_tn(v, p.astype(jnp.bfloat16))

    @pl.when(jnp.logical_not(own))
    def _():
        top_ref[...] = jnp.full(top_ref.shape, FAR, jnp.float32)
        sum_ref[...] = jnp.zeros(sum_ref.shape, jnp.float32)
        acc_ref[...] = jnp.zeros(acc_ref.shape, jnp.float32)

    def advance(t, carry):
        blocks = [block(list_ref[t * STEP + u]) for u in range(STEP)]
        v = jnp.concatenate([b[1] for b in blocks], axis=0)
        s = dot_nt(jnp.concatenate([b[0] for b in blocks], axis=0), qs)
        s = jnp.concatenate(
            [
                jnp.where(t * STEP + u < count, s[u * LONG_DEV : (u + 1) * LONG_DEV], FAR)
                for u in range(STEP)
            ],
            axis=0,
        )
        old = top_ref[...]
        new = jnp.maximum(old, jnp.max(s, axis=0, keepdims=True))
        p = jnp.exp2((s - new) * SCALE2)
        factor = jnp.exp2((old - new) * SCALE2)
        top_ref[...] = new
        sum_ref[...] = sum_ref[...] * factor + jnp.sum(p, axis=0, keepdims=True)
        acc_ref[...] = acc_ref[...] * factor + dot_tn(v, p.astype(jnp.bfloat16))
        return carry

    lax.fori_loop(0, (count + STEP - 1) // STEP, advance, 0)
    total = sum_ref[...]
    o = acc_ref[...] / jnp.where(total > 0.0, total, 1.0)
    out_ref[0, :HEAD] = o.astype(jnp.bfloat16)
    parts = (*three_parts(top_ref[...] * SCALE2), *three_parts(total))
    row = lax.broadcasted_iota(jnp.int32, (STATS, cols), 0)
    stats = jnp.zeros((STATS, cols), jnp.float32)
    for i, part in enumerate(parts):
        stats = jnp.where(row == i, part, stats)
    out_ref[0, HEAD:] = stats.astype(jnp.bfloat16)


def merged_rows(got_ref):
    tops, sums = [], []
    for j in range(got_ref.shape[0]):
        stats = got_ref[j, HEAD:].astype(jnp.float32)
        tops.append(stats[0:1] + stats[1:2] + stats[2:3])
        sums.append(stats[3:4] + stats[4:5] + stats[5:6])
    top = jnp.maximum(jnp.maximum(tops[0], tops[1]), jnp.maximum(tops[2], tops[3]))
    shares = [s * jnp.exp2(t - top) for s, t in zip(sums, tops)]
    total = (shares[0] + shares[1]) + (shares[2] + shares[3])
    o = got_ref[0, :HEAD].astype(jnp.float32) * (shares[0] / total)
    for j in range(1, 4):
        o = o + got_ref[j, :HEAD].astype(jnp.float32) * (shares[j] / total)
    return heads_across(o).astype(jnp.bfloat16)


def projector(make_rows):
    def kernel(core_ref, *refs):
        *inputs, weight_ref, send_ref, keep_ref, rows_ref = refs
        half = rows_ref.shape[0] // 2

        @pl.when(pl.program_id(0) == 0)
        def _():
            made = make_rows(*inputs)
            core = core_ref[0]
            for b in range(2):
                at = pl.multiple_of(jnp.where(core == b, half, 0), half)
                rows_ref[pl.ds(at, half), :] = made[b * half : (b + 1) * half]

        product = jnp.dot(rows_ref[...], weight_ref[...], preferred_element_type=jnp.float32)
        rounded = product.astype(jnp.bfloat16)
        send_ref[...] = rounded[:half]
        keep_ref[...] = rounded[half:]

    return kernel


def project(make_rows, core, inputs, weight, name):
    cols, width = weight.shape
    half = LONG_DEV // 2
    block = 1024
    out = pl.BlockSpec((half, block), lambda i, c: (0, i))
    shape = jax.ShapeDtypeStruct((half, width), jnp.bfloat16)
    return pl.pallas_call(
        projector(make_rows),
        grid_spec=pltpu.PrefetchScalarGridSpec(
            num_scalar_prefetch=1,
            grid=(width // block,),
            in_specs=[
                *[pl.BlockSpec(memory_space=pltpu.VMEM) for _ in inputs],
                pl.BlockSpec((cols, block), lambda i, c: (0, i)),
            ],
            out_specs=[out, out],
            scratch_shapes=[pltpu.VMEM((2 * half, cols), jnp.bfloat16)],
        ),
        out_shape=(shape, shape),
        name=name,
    )(core, *inputs, weight)


def pair_sum(a, b):
    return (a.astype(jnp.float32) + b.astype(jnp.float32)).astype(jnp.bfloat16)


def route_kernel(
    level_ref,
    res_ref,
    keep_ref,
    near_ref,
    far_ref,
    short_ref,
    gain_ref,
    owner_ref,
    hidden_ref,
    out_ref,
    wide_ref,
):
    long = (keep_ref[...].astype(jnp.float32) + near_ref[...].astype(jnp.float32)) + far_ref[
        ...
    ].astype(jnp.float32)
    summed = jnp.where(level_ref[0] == 0, long, short_ref[...])
    hidden = (res_ref[...].astype(jnp.float32) + summed).astype(jnp.bfloat16)
    hidden_ref[...] = hidden
    h = hidden.astype(jnp.float32)
    mean = jnp.mean(h * h, axis=1, keepdims=True)
    normed = (h * lax.rsqrt(mean + 1e-05) * gain_ref[...].astype(jnp.float32)).astype(jnp.bfloat16)
    rows = h.shape[0]
    down = jnp.broadcast_to(owner_ref[...].astype(jnp.float32), (rows, HEAD))
    across = down.T[:rows]
    row = lax.broadcasted_iota(jnp.int32, (rows, rows), 0)
    col = lax.broadcasted_iota(jnp.int32, (rows, rows), 1)
    same = (down[:, :rows] == across) & (row < col)
    slot = jnp.sum(jnp.where(same, 1.0, 0.0), axis=0, keepdims=True)
    mine = across == row.astype(jnp.float32)
    owners = rows
    stride = out_ref.shape[0] // owners
    for s in range(2):
        pick = jnp.where(mine & (slot == float(s)), 1.0, 0.0).astype(jnp.bfloat16)
        placed = jnp.dot(pick, normed, preferred_element_type=jnp.float32)
        for t in range(stride // 2):
            wide_ref[pl.ds(2 * t + s, owners, stride=stride), :] = placed[
                :, t * HEAD : (t + 1) * HEAD
            ]
    out_ref[...] = wide_ref[...].astype(jnp.bfloat16)


def in_vmem(x):
    return pltpu.with_memory_space_constraint(x, pltpu.VMEM)


def exchange(x, groups=None):
    return lax.all_to_all(x, "wide", 0, 0, tiled=True, axis_index_groups=groups)


def on_device(
    queries, key_rows, value_rows, residual, out_weight, norm_gain, span_map, segments, row_owner
):
    wide = lax.axis_index("wide").astype(jnp.int32).reshape(1)
    narrow = lax.axis_index("narrow").astype(jnp.int32).reshape(1)
    core = narrow & 1
    level = lax.shift_right_logical(narrow, jnp.ones_like(narrow))
    bf = jnp.bfloat16
    cols = queries.shape[1]
    width = out_weight.shape[1]
    vmem = pl.BlockSpec(memory_space=pltpu.VMEM)
    kv, qs = pl.pallas_call(
        prep_kernel,
        out_shape=(
            jax.ShapeDtypeStruct((16, LONG_DEV, 2 * HEAD), bf),
            jax.ShapeDtypeStruct((4, LONG_DEV, cols), bf),
        ),
        name="prep",
    )(queries, key_rows, value_rows)
    across = [(0, 1), (1, 0), (2, 3), (3, 2)]
    kv, qs, core_after = lax.optimization_barrier((kv, qs, core))
    kv = exchange(kv, KEY_GROUPS)
    qs = exchange(qs, QUERY_GROUPS)
    send, keep_short = project(
        short_rows, core_after, (queries, key_rows, value_rows, segments), out_weight, "short"
    )
    near_short = lax.ppermute(send, "narrow", across)
    pair_short = pair_sum(keep_short, near_short)
    far_short = lax.ppermute(pair_short, "narrow", [(0, 2), (1, 3)])
    short = (keep_short.astype(jnp.float32) + near_short.astype(jnp.float32)) + far_short.astype(
        jnp.float32
    )
    wide, short = lax.optimization_barrier((wide, short))
    parts = pl.pallas_call(
        attend_kernel,
        grid_spec=pltpu.PrefetchScalarGridSpec(
            num_scalar_prefetch=2,
            grid=(4,),
            in_specs=[vmem, pl.BlockSpec((16, LONG_DEV, 2 * HEAD), lambda j, w, m: (0, 0, 0))],
            out_specs=pl.BlockSpec((1, HEAD + STATS, cols), lambda j, w, m: (j, 0, 0)),
            scratch_shapes=[
                pltpu.SMEM((16 + STEP,), jnp.int32),
                pltpu.VMEM((1, cols), jnp.float32),
                pltpu.VMEM((1, cols), jnp.float32),
                pltpu.VMEM((HEAD, cols), jnp.float32),
            ],
        ),
        out_shape=jax.ShapeDtypeStruct((4, HEAD + STATS, cols), bf),
        name="attend",
    )(wide, span_map, in_vmem(qs), kv)
    got = exchange(parts, QUERY_GROUPS)
    send, keep = project(merged_rows, core, (in_vmem(got),), out_weight, "long")
    near = lax.ppermute(send, "narrow", across)
    far = lax.ppermute(pair_sum(keep, near), "narrow", [(2, 0), (3, 1)])
    rows = residual.shape[0]
    owners = 64
    tiles = 2 * width // HEAD
    hidden, outgoing = pl.pallas_call(
        route_kernel,
        in_specs=[pl.BlockSpec(memory_space=pltpu.SMEM)] + [vmem] * 7,
        out_shape=(
            jax.ShapeDtypeStruct((rows, width), bf),
            jax.ShapeDtypeStruct((owners * tiles, HEAD), bf),
        ),
        scratch_shapes=[pltpu.VMEM((owners * tiles, HEAD), jnp.float32)],
        name="route",
    )(level, residual, keep, in_vmem(near), in_vmem(far), in_vmem(short), norm_gain.reshape(1, width), row_owner)
    arrived = exchange(outgoing.reshape(owners, tiles, HEAD))
    arrived = arrived.reshape(owners, tiles // 2, 2, HEAD).transpose(0, 2, 1, 3)
    return (hidden, arrived.reshape(1, 1, owners, 2, width))


def solution(mesh):
    placed = (
        P(("rep", "wide"), "narrow"),
        P(("rep", "wide"), "narrow"),
        P(("rep", "wide"), "narrow"),
        P(("rep", "wide", "narrow"), None),
        P("narrow", None),
        P(),
        P(),
        P(("rep", "wide"), None),
        P(("rep", "wide", "narrow"), None),
    )
    return jax.shard_map(
        on_device,
        mesh=mesh,
        in_specs=placed,
        out_specs=(
            P(("rep", "wide", "narrow"), None),
            P(("rep", "wide"), "narrow", None, None, None),
        ),
        check_vma=False,
    )
```

time: 166 us -> 162 us (0.976)
  the two profiles are of different devices: /device:TPU:288 before, /device:TPU:32 now
where the time goes in v2:
time: 162 us
  blocking collectives  56.4 us (35%)
  waiting for transfers between devices  42.8 us (26%)
  Pallas kernels  27.5 us (17%)
  starting transfers between devices  27.4 us (17%)
  other arithmetic  3.7 us (2%)
  local copies, waits for them, and re-layouts  3.64 us (2%)
    all_to_all x2, blocking collectives, exchange(): return lax.all_to_all(x, 'wide', 0, 0, tiled=True, axis_index_groups=groups)  56.4 us
    all_to_all x2, starting transfers between devices, exchange(): return lax.all_to_all(x, 'wide', 0, 0, tiled=True, axis_index_groups=groups)  18.8 us
    all_to_all x2, waiting for transfers between devices, exchange(): return lax.all_to_all(x, 'wide', 0, 0, tiled=True, axis_index_groups=groups)  17.9 us
    ppermute x1, waiting for transfers between devices, on_device(): far = lax.ppermute(pair_sum(keep, near), 'narrow', [(2, 0), (3, 1)])  13.2 us
    pallas_call x1, Pallas kernels, on_device(): pl.pallas_call(attend_kernel, grid_spec=pltpu.PrefetchScalarGridSpec(num_...  11.2 us
    pallas_call x2, Pallas kernels, project(): pl.pallas_call(projector(make_rows), grid_spec=pltpu.PrefetchScalarGridSp...  9.9 us
    ppermute x1, waiting for transfers between devices, on_device(): far_short = lax.ppermute(pair_short, 'narrow', [(0, 2), (1, 3)])  9.57 us
    pallas_call x1, Pallas kernels, on_device(): pl.pallas_call(route_kernel, in_specs=[pl.BlockSpec(memory_space=pltpu.SM...  4.19 us
  transfers between devices with their start and end apart: 6, of which 5 were waited for; matrix products, arithmetic and copies ran while one was open for 2% of the time, Pallas kernels for 3%

profile of v2, /device:TPU:32, one launch (start us, length us, event | category | flops | bytes accessed | tf_op | source)
XLA Modules:
  0.0 162.1 jit_solution(8209511470584996657)
XLA Ops:
  0.6 2.2 %prep.1 = (bf16[16,128,256]{2,1,0:T(8,128)(2,1)}, bf16[4,128,512]{2,1,0:T(8,128)(2,1)}) custom-call(bf16[256,512]{1,0:T(8,128)(2,1)} %refs_0_.1, bf16[256,128]{1,0:T(8,128)(2,1)} %refs_1_.2, bf16[256,128]{1,0:T(8,128)(2,1)} %refs_2_.1), custom_call_target="tpu_custom_call" | custom-call | tf_op jit(solution)/shard_map/prep/pallas_call | solution.py:279
  2.9 3.9 %all-to-all-start = ((bf16[4,128,512]{2,1,0:T(8,128)(2,1)}), bf16[4,128,512]{2,1,0:T(8,128)(2,1)S(1)}, u32[]{:S(2)}, u32[]{:S(2)}) async-start(bf16[4,128,512]{2,1,0:T(8,128)(2,1)} %get-tuple-element.21), calls=%async_computation | async-start | bytes 1048576 | tf_op jit(solution)/shard_map/all_to_all | solution.py:265
  6.8 5.1 %short.1 = (bf16[64,4096]{1,0:T(8,128)(2,1)}, bf16[64,4096]{1,0:T(8,128)(2,1)}) custom-call(s32[1]{0:T(128)} %bitcast.1.core_ref, bf16[256,512]{1,0:T(8,128)(2,1)} %refs_0_.1, bf16[256,128]{1,0:T(8,128)(2,1)} %refs_1_.2, bf16[256,128]{1,0:T(8,128)(2,1)} %refs_2_.1, s32[1,128]{1,0:T(1,128)} %refs_3_.1, bf16[512,4096]{1,0:T(8,128)(2,1)} %refs_1_.3), custom_call_target="tpu_custom_call" | custom-call | tf_op jit(solution)/shard_map/short/pallas_call | solution.py:197
  11.9 1.9 %collective-permute-start = (bf16[64,4096]{1,0:T(8,128)(2,1)}, bf16[64,4096]{1,0:T(8,128)(2,1)S(1)}, u32[]{:S(2)}, u32[]{:S(2)}) collective-permute-start(bf16[64,4096]{1,0:T(8,128)(2,1)} %get-tuple-element.19), channel_id=1, source_target_pairs={{0,4},{4,0},{8,12},{12,8},{1,5},{5,1},{9,13},{13,9},{2,6},{6,2},{1... | collective-permute-start | bytes 1572872 | tf_op jit(solution)/shard_map/ppermute | solution.py:294
  13.8 1.0 all-to-all-done.q_ref
  14.8 14.9 %all-to-all-start.1 = ((bf16[16,128,256]{2,1,0:T(8,128)(2,1)}), bf16[16,128,256]{2,1,0:T(8,128)(2,1)S(1)}, u32[]{:S(2)}, u32[]{:S(2)}) async-start(bf16[16,128,256]{2,1,0:T(8,128)(2,1)} %get-tuple-element.22), calls=%async_computation.1 | async-start | bytes 2097152 | tf_op jit(solution)/shard_map/all_to_all | solution.py:265
  29.7 1.2 fusion
  30.8 3.6 %collective-permute-start.1 = (bf16[64,4096]{1,0:T(8,128)(2,1)S(1)}, bf16[64,4096]{1,0:T(8,128)(2,1)}, u32[]{:S(2)}, u32[]{:S(2)}) collective-permute-start(bf16[64,4096]{1,0:T(8,128)(2,1)S(1)} %fusion), channel_id=1, source_target_pairs={{0,8},{4,12},{1,9},{5,13},{2,10},{6,14},{3,11},{7,15},{16,24},{20,... | collective-permute-start | bytes 1572872 | tf_op jit(solution)/shard_map/ppermute | solution.py:296
  34.4 9.6 %collective-permute-done.1 = bf16[64,4096]{1,0:T(8,128)(2,1)} collective-permute-done((bf16[64,4096]{1,0:T(8,128)(2,1)S(1)}, bf16[64,4096]{1,0:T(8,128)(2,1)}, u32[]{:S(2)}, u32[]{:S(2)}) %collective-permute-start.1) | collective-permute-done | bytes 524320 | tf_op jit(solution)/shard_map/ppermute | solution.py:296
  44.0 1.4 convert_add_fusion.short_ref
  45.3 16.9 %all-to-all-done.1.kv_ref = bf16[16,128,256]{2,1,0:T(8,128)(2,1)S(1)} async-done(((bf16[16,128,256]{2,1,0:T(8,128)(2,1)}), bf16[16,128,256]{2,1,0:T(8,128)(2,1)S(1)}, u32[]{:S(2)}, u32[]{:S(2)}) %all-to-all-start.1) | async-done | bytes 1048608 | tf_op jit(solution)/shard_map/all_to_all | solution.py:265
  62.3 1.0 copy-done
  63.2 11.2 %attend.1 = bf16[4,144,512]{2,1,0:T(8,128)(2,1)} custom-call(s32[1]{0:T(128)} %bitcast.2.wide_ref, s32[64]{0:T(128)} %span_ref.1, bf16[4,128,512]{2,1,0:T(8,128)(2,1)S(1)} %all-to-all-done.q_ref, bf16[16,128,256]{2,1,0:T(8,128)(2,1)} %copy-done), custom_call_target="tpu_custom_call" | custom-call | tf_op jit(solution)/shard_map/attend/pallas_call | solution.py:301
  74.4 12.8 %all_to_all.20.refs_0_ = bf16[4,144,512]{2,1,0:T(8,128)(2,1)S(1)} all-to-all(bf16[4,144,512]{2,1,0:T(8,128)(2,1)} %attend.1), channel_id=1, replica_groups={{0,16,128,144},{32,48,160,176},{64,80,192,208},{96,112,224,240},{256,27..., dimensions={0} | all-to-all | bytes 1179648 | tf_op jit(solution)/shard_map/all_to_all | solution.py:265
  87.2 4.8 %long.1 = (bf16[64,4096]{1,0:T(8,128)(2,1)}, bf16[64,4096]{1,0:T(8,128)(2,1)}) custom-call(s32[1]{0:T(128)} %bitcast.1.core_ref, bf16[4,144,512]{2,1,0:T(8,128)(2,1)S(1)} %all_to_all.20.refs_0_, bf16[512,4096]{1,0:T(8,128)(2,1)} %refs_1_.3), custom_call_target="tpu_custom_call" | custom-call | tf_op jit(solution)/shard_map/long/pallas_call | solution.py:197
  92.0 1.9 %collective-permute-start.2 = (bf16[64,4096]{1,0:T(8,128)(2,1)}, bf16[64,4096]{1,0:T(8,128)(2,1)S(1)}, u32[]{:S(2)}, u32[]{:S(2)}) collective-permute-start(bf16[64,4096]{1,0:T(8,128)(2,1)} %get-tuple-element.24), channel_id=1, source_target_pairs={{0,4},{4,0},{8,12},{12,8},{1,5},{5,1},{9,13},{13,9},{2,6},{6,2},{1... | collective-permute-start | bytes 1572872 | tf_op jit(solution)/shard_map/ppermute | solution.py:320
  93.9 2.1 %collective-permute-done.2.near_ref = bf16[64,4096]{1,0:T(8,128)(2,1)S(1)} collective-permute-done((bf16[64,4096]{1,0:T(8,128)(2,1)}, bf16[64,4096]{1,0:T(8,128)(2,1)S(1)}, u32[]{:S(2)}, u32[]{:S(2)}) %collective-permute-start.2) | collective-permute-done | bytes 524320 | tf_op jit(solution)/shard_map/ppermute | solution.py:320
  96.0 1.2 add_convert_fusion
  97.1 1.3 collective-permute-start.3
  98.4 0.7 copy.11.owner_ref
  99.8 13.2 %collective-permute-done.3.far_ref = bf16[64,4096]{1,0:T(8,128)(2,1)S(1)} collective-permute-done((bf16[64,4096]{1,0:T(8,128)(2,1)S(1)}, bf16[64,4096]{1,0:T(8,128)(2,1)S(1)}, u32[]{:S(2)}, u32[]{:S(2)}) %collective-permute-start.3) | collective-permute-done | bytes 524320 | tf_op jit(solution)/shard_map/ppermute | solution.py:321
  113.0 4.2 %route.1 = (bf16[64,4096]{1,0:T(8,128)(2,1)}, bf16[4096,128]{1,0:T(8,128)(2,1)}) custom-call(s32[1]{0:T(128)} %bitcast.level_ref, bf16[64,4096]{1,0:T(8,128)(2,1)} %res_ref.1, bf16[64,4096]{1,0:T(8,128)(2,1)} %get-tuple-element.23.keep_ref, bf16[64,4096]{1,0:T(8,128)(2,1)S(1)} %collective-permute-done.2.near_ref, ...), custom_call_target="tpu_custom_call" | custom-call | tf_op jit(solution)/shard_map/route/pallas_call | solution.py:325
  117.2 43.5 %all_to_all.21 = bf16[64,64,128]{2,1,0:T(8,128)(2,1)S(1)} all-to-all(bf16[64,64,128]{2,1,0:T(8,128)(2,1)} %bitcast.12), channel_id=1, replica_groups=mesh['wide'=64,'narrow'=4,'rep'=4] {'wide'}, dimensions={0} | all-to-all | bytes 2097152 | tf_op jit(solution)/shard_map/all_to_all | solution.py:265
  161.0 1.1 reshape.28
  (8 shorter events, 0.9 us)
Async XLA Ops:
  2.9 11.9 %all-to-all-start = ((bf16[4,128,512]{2,1,0:T(8,128)(2,1)}), bf16[4,128,512]{2,1,0:T(8,128)(2,1)S(1)}, u32[]{:S(2)}, u32[]{:S(2)}) async-start(bf16[4,128,512]{2,1,0:T(8,128)(2,1)} %get-tuple-element.21), calls=%async_computation | async-start | bytes 1048576 | tf_op jit(solution)/shard_map/all_to_all | solution.py:265
  11.9 17.8 %collective-permute-start = (bf16[64,4096]{1,0:T(8,128)(2,1)}, bf16[64,4096]{1,0:T(8,128)(2,1)S(1)}, u32[]{:S(2)}, u32[]{:S(2)}) collective-permute-start(bf16[64,4096]{1,0:T(8,128)(2,1)} %get-tuple-element.19), channel_id=1, source_target_pairs={{0,4},{4,0},{8,12},{12,8},{1,5},{5,1},{9,13},{13,9},{2,6},{6,2},{1... | collective-permute-start | bytes 1572872 | tf_op jit(solution)/shard_map/ppermute | solution.py:294
  14.8 47.5 %all-to-all-start.1 = ((bf16[16,128,256]{2,1,0:T(8,128)(2,1)}), bf16[16,128,256]{2,1,0:T(8,128)(2,1)S(1)}, u32[]{:S(2)}, u32[]{:S(2)}) async-start(bf16[16,128,256]{2,1,0:T(8,128)(2,1)} %get-tuple-element.22), calls=%async_computation.1 | async-start | bytes 2097152 | tf_op jit(solution)/shard_map/all_to_all | solution.py:265
  30.8 13.1 %collective-permute-start.1 = (bf16[64,4096]{1,0:T(8,128)(2,1)S(1)}, bf16[64,4096]{1,0:T(8,128)(2,1)}, u32[]{:S(2)}, u32[]{:S(2)}) collective-permute-start(bf16[64,4096]{1,0:T(8,128)(2,1)S(1)} %fusion), channel_id=1, source_target_pairs={{0,8},{4,12},{1,9},{5,13},{2,10},{6,14},{3,11},{7,15},{16,24},{20,... | collective-permute-start | bytes 1572872 | tf_op jit(solution)/shard_map/ppermute | solution.py:296
  62.3 1.0 copy-start
  74.4 24.0 %copy-start.2 = (s32[64,1]{0,1:T(1,128)S(1)}, s32[64,1]{0,1:T(1,128)}, u32[]{:S(2)}) copy-start(s32[64,1]{0,1:T(1,128)} %param.17) | copy-start | bytes 772
  74.4 24.8 %copy-start.1 = (bf16[4096]{0:T(1024)(128)(2,1)S(1)}, bf16[4096]{0:T(1024)(128)(2,1)}, u32[]{:S(2)}) copy-start(bf16[4096]{0:T(1024)(128)(2,1)} %param.14) | copy-start | bytes 24580
  92.0 4.0 %collective-permute-start.2 = (bf16[64,4096]{1,0:T(8,128)(2,1)}, bf16[64,4096]{1,0:T(8,128)(2,1)S(1)}, u32[]{:S(2)}, u32[]{:S(2)}) collective-permute-start(bf16[64,4096]{1,0:T(8,128)(2,1)} %get-tuple-element.24), channel_id=1, source_target_pairs={{0,4},{4,0},{8,12},{12,8},{1,5},{5,1},{9,13},{13,9},{2,6},{6,2},{1... | collective-permute-start | bytes 1572872 | tf_op jit(solution)/shard_map/ppermute | solution.py:320
  97.1 15.9 %collective-permute-start.3 = (bf16[64,4096]{1,0:T(8,128)(2,1)S(1)}, bf16[64,4096]{1,0:T(8,128)(2,1)S(1)}, u32[]{:S(2)}, u32[]{:S(2)}) collective-permute-start(bf16[64,4096]{1,0:T(8,128)(2,1)S(1)} %add_convert_fusion), channel_id=1, source_target_pairs={{8,0},{12,4},{9,1},{13,5},{10,2},{14,6},{11,3},{15,7},{24,16},{28,... | collective-permute-start | bytes 1572872 | tf_op jit(solution)/shard_map/ppermute | solution.py:321

commit v3 on v2

--- a/solution.py
+++ b/solution.py
@@ -11,6 +11,7 @@
 HEADS = 4
 SCALE = HEAD ** (-0.5)
 FAR = -1e30
+ROOM = pltpu.CompilerParams(vmem_limit_bytes=24 * 1024 * 1024)
 STATS = 16
 STEP = 4
 SCALE2 = SCALE * 1.4426950408889634
@@ -34,6 +35,10 @@
     return lax.dot_general(a, b, (((0,), (0,)), ((), ())), preferred_element_type=jnp.float32)
 
 
+def dot(a, b):
+    return jnp.dot(a, b, preferred_element_type=jnp.float32)
+
+
 def heads_down(q):
     return jnp.concatenate([q[:, h * HEAD : (h + 1) * HEAD] for h in range(HEADS)], axis=0)
 
@@ -45,10 +50,10 @@
 
 
 def prep_kernel(q_ref, k_ref, v_ref, kv_out, q_out):
-    kv = jnp.concatenate([k_ref[:LONG_DEV], v_ref[:LONG_DEV]], axis=1)
+    kv = jnp.concatenate([k_ref[:LONG_DEV], v_ref[:LONG_DEV].T], axis=1)
     for i in range(kv_out.shape[0]):
         kv_out[i] = kv
-    q = q_ref[:LONG_DEV]
+    q = heads_across(q_ref[:LONG_DEV])
     for j in range(q_out.shape[0]):
         q_out[j] = q
 
@@ -88,8 +93,9 @@
     y = w // SIDE
     x = w % SIDE
     q_span = span_ref[((y // 2) * 2 + j // 2) * SIDE + (x // 2) * 2 + j % 2]
-    qs = heads_down(q_ref[j])
-    cols = qs.shape[0]
+    qs = q_ref[j]
+    cols = qs.shape[1]
+    half = cols // 2
     count = jnp.int32(0)
     for i in range(kv_ref.shape[0]):
         span = span_ref[((i // 4) * 2 + y % 2) * SIDE + (i % 4) * 2 + x % 2]
@@ -99,20 +105,17 @@
         list_ref[count + i] = 0
     own = j == (y % 2) * 2 + x % 2
 
-    def block(i):
-        return kv_ref[i, :, :HEAD], kv_ref[i, :, HEAD:]
-
     @pl.when(own)
     def _():
-        k, v = block((y // 2) * 4 + x // 2)
+        kv = kv_ref[(y // 2) * 4 + x // 2]
         row = lax.broadcasted_iota(jnp.int32, (LONG_DEV, cols), 0)
         col = lax.broadcasted_iota(jnp.int32, (LONG_DEV, cols), 1)
-        s = jnp.where(row <= col % LONG_DEV, dot_nt(k, qs), FAR)
+        s = jnp.where(row <= col % LONG_DEV, dot(kv[:, :HEAD], qs), FAR)
         top = jnp.max(s, axis=0, keepdims=True)
         p = jnp.exp2((s - top) * SCALE2)
         top_ref[...] = top
         sum_ref[...] = jnp.sum(p, axis=0, keepdims=True)
-        acc_ref[...] = dot_tn(v, p.astype(jnp.bfloat16))
+        acc_ref[...] = dot(kv[:, HEAD:], p.astype(jnp.bfloat16))
 
     @pl.when(jnp.logical_not(own))
     def _():
@@ -120,27 +123,39 @@
         sum_ref[...] = jnp.zeros(sum_ref.shape, jnp.float32)
         acc_ref[...] = jnp.zeros(acc_ref.shape, jnp.float32)
 
-    def advance(t, carry):
-        blocks = [block(list_ref[t * STEP + u]) for u in range(STEP)]
-        v = jnp.concatenate([b[1] for b in blocks], axis=0)
-        s = dot_nt(jnp.concatenate([b[0] for b in blocks], axis=0), qs)
-        s = jnp.concatenate(
-            [
-                jnp.where(t * STEP + u < count, s[u * LONG_DEV : (u + 1) * LONG_DEV], FAR)
-                for u in range(STEP)
-            ],
-            axis=0,
-        )
-        old = top_ref[...]
-        new = jnp.maximum(old, jnp.max(s, axis=0, keepdims=True))
-        p = jnp.exp2((s - new) * SCALE2)
-        factor = jnp.exp2((old - new) * SCALE2)
-        top_ref[...] = new
-        sum_ref[...] = sum_ref[...] * factor + jnp.sum(p, axis=0, keepdims=True)
-        acc_ref[...] = acc_ref[...] * factor + dot_tn(v, p.astype(jnp.bfloat16))
+    def advance(t, last):
+        ids = [list_ref[t * STEP + u] for u in range(STEP)]
+        k = jnp.concatenate([kv_ref[i, :, :HEAD] for i in ids], axis=0)
+        v = jnp.concatenate([kv_ref[i, :, HEAD:] for i in ids], axis=1)
+        scores = [dot(k, qs[:, g * half : (g + 1) * half]) for g in range(2)]
+        for g, s in enumerate(scores):
+            if last:
+                s = jnp.concatenate(
+                    [
+                        jnp.where(t * STEP + u < count, s[u * LONG_DEV : (u + 1) * LONG_DEV], FAR)
+                        for u in range(STEP)
+                    ],
+                    axis=0,
+                )
+            at = slice(g * half, (g + 1) * half)
+            old = top_ref[:, at]
+            new = jnp.maximum(old, jnp.max(s, axis=0, keepdims=True))
+            p = jnp.exp2((s - new) * SCALE2)
+            factor = jnp.exp2((old - new) * SCALE2)
+            top_ref[:, at] = new
+            sum_ref[:, at] = sum_ref[:, at] * factor + jnp.sum(p, axis=0, keepdims=True)
+            acc_ref[:, at] = acc_ref[:, at] * factor + dot(v, p.astype(jnp.bfloat16))
+
+    def step(t, carry):
+        advance(t, False)
         return carry
 
-    lax.fori_loop(0, (count + STEP - 1) // STEP, advance, 0)
+    lax.fori_loop(0, count // STEP, step, 0)
+
+    @pl.when(count % STEP > 0)
+    def _():
+        advance(count // STEP, True)
+
     total = sum_ref[...]
     o = acc_ref[...] / jnp.where(total > 0.0, total, 1.0)
     out_ref[0, :HEAD] = o.astype(jnp.bfloat16)
@@ -180,7 +195,7 @@
                 at = pl.multiple_of(jnp.where(core == b, half, 0), half)
                 rows_ref[pl.ds(at, half), :] = made[b * half : (b + 1) * half]
 
-        product = jnp.dot(rows_ref[...], weight_ref[...], preferred_element_type=jnp.float32)
+        product = dot(rows_ref[...], weight_ref[...])
         rounded = product.astype(jnp.bfloat16)
         send_ref[...] = rounded[:half]
         keep_ref[...] = rounded[half:]
@@ -188,7 +203,11 @@
     return kernel
 
 
-def project(make_rows, core, inputs, weight, name):
+def whole(x):
+    return pl.BlockSpec(x.shape, lambda *i: (0,) * x.ndim)
+
+
+def project(make_rows, core, inputs, specs, weight, name):
     cols, width = weight.shape
     half = LONG_DEV // 2
     block = 1024
@@ -200,7 +219,7 @@
             num_scalar_prefetch=1,
             grid=(width // block,),
             in_specs=[
-                *[pl.BlockSpec(memory_space=pltpu.VMEM) for _ in inputs],
+                *specs,
                 pl.BlockSpec((cols, block), lambda i, c: (0, i)),
             ],
             out_specs=[out, out],
@@ -215,24 +234,8 @@
     return (a.astype(jnp.float32) + b.astype(jnp.float32)).astype(jnp.bfloat16)
 
 
-def route_kernel(
-    level_ref,
-    res_ref,
-    keep_ref,
-    near_ref,
-    far_ref,
-    short_ref,
-    gain_ref,
-    owner_ref,
-    hidden_ref,
-    out_ref,
-    wide_ref,
-):
-    long = (keep_ref[...].astype(jnp.float32) + near_ref[...].astype(jnp.float32)) + far_ref[
-        ...
-    ].astype(jnp.float32)
-    summed = jnp.where(level_ref[0] == 0, long, short_ref[...])
-    hidden = (res_ref[...].astype(jnp.float32) + summed).astype(jnp.bfloat16)
+def route_kernel(base_ref, far_ref, gain_ref, owner_ref, hidden_ref, out_ref, wide_ref):
+    hidden = (base_ref[...] + far_ref[...].astype(jnp.float32)).astype(jnp.bfloat16)
     hidden_ref[...] = hidden
     h = hidden.astype(jnp.float32)
     mean = jnp.mean(h * h, axis=1, keepdims=True)
@@ -251,7 +254,7 @@
         pick = jnp.where(mine & (slot == float(s)), 1.0, 0.0).astype(jnp.bfloat16)
         placed = jnp.dot(pick, normed, preferred_element_type=jnp.float32)
         for t in range(stride // 2):
-            wide_ref[pl.ds(2 * t + s, owners, stride=stride), :] = placed[
+            wide_ref[pl.ds(s * (stride // 2) + t, owners, stride=stride), :] = placed[
                 :, t * HEAD : (t + 1) * HEAD
             ]
     out_ref[...] = wide_ref[...].astype(jnp.bfloat16)
@@ -278,6 +281,12 @@
     vmem = pl.BlockSpec(memory_space=pltpu.VMEM)
     kv, qs = pl.pallas_call(
         prep_kernel,
+        grid=(1,),
+        in_specs=[whole(x) for x in (queries, key_rows, value_rows)],
+        out_specs=(
+            pl.BlockSpec((16, LONG_DEV, 2 * HEAD), lambda i: (0, 0, 0)),
+            pl.BlockSpec((4, LONG_DEV, cols), lambda i: (0, 0, 0)),
+        ),
         out_shape=(
             jax.ShapeDtypeStruct((16, LONG_DEV, 2 * HEAD), bf),
             jax.ShapeDtypeStruct((4, LONG_DEV, cols), bf),
@@ -288,8 +297,9 @@
     kv, qs, core_after = lax.optimization_barrier((kv, qs, core))
     kv = exchange(kv, KEY_GROUPS)
     qs = exchange(qs, QUERY_GROUPS)
+    short_in = (queries, key_rows, value_rows, segments)
     send, keep_short = project(
-        short_rows, core_after, (queries, key_rows, value_rows, segments), out_weight, "short"
+        short_rows, core_after, short_in, [whole(x) for x in short_in], out_weight, "short"
     )
     near_short = lax.ppermute(send, "narrow", across)
     pair_short = pair_sum(keep_short, near_short)
@@ -303,7 +313,7 @@
         grid_spec=pltpu.PrefetchScalarGridSpec(
             num_scalar_prefetch=2,
             grid=(4,),
-            in_specs=[vmem, pl.BlockSpec((16, LONG_DEV, 2 * HEAD), lambda j, w, m: (0, 0, 0))],
+            in_specs=[vmem, vmem],
             out_specs=pl.BlockSpec((1, HEAD + STATS, cols), lambda j, w, m: (j, 0, 0)),
             scratch_shapes=[
                 pltpu.SMEM((16 + STEP,), jnp.int32),
@@ -314,26 +324,30 @@
         ),
         out_shape=jax.ShapeDtypeStruct((4, HEAD + STATS, cols), bf),
         name="attend",
-    )(wide, span_map, in_vmem(qs), kv)
+        compiler_params=ROOM,
+    )(wide, span_map, in_vmem(qs), in_vmem(kv))
     got = exchange(parts, QUERY_GROUPS)
-    send, keep = project(merged_rows, core, (in_vmem(got),), out_weight, "long")
+    send, keep = project(merged_rows, core, (in_vmem(got),), [vmem], out_weight, "long")
     near = lax.ppermute(send, "narrow", across)
-    far = lax.ppermute(pair_sum(keep, near), "narrow", [(2, 0), (3, 1)])
+    pair, keep, near = lax.optimization_barrier((pair_sum(keep, near), keep, near))
+    far = lax.ppermute(pair, "narrow", [(2, 0), (3, 1)])
+    long = keep.astype(jnp.float32) + near.astype(jnp.float32)
+    base = residual.astype(jnp.float32) + jnp.where(level[0] == 0, long, short)
     rows = residual.shape[0]
     owners = 64
     tiles = 2 * width // HEAD
     hidden, outgoing = pl.pallas_call(
         route_kernel,
-        in_specs=[pl.BlockSpec(memory_space=pltpu.SMEM)] + [vmem] * 7,
+        in_specs=[vmem] * 4,
         out_shape=(
             jax.ShapeDtypeStruct((rows, width), bf),
             jax.ShapeDtypeStruct((owners * tiles, HEAD), bf),
         ),
         scratch_shapes=[pltpu.VMEM((owners * tiles, HEAD), jnp.float32)],
         name="route",
-    )(level, residual, keep, in_vmem(near), in_vmem(far), in_vmem(short), norm_gain.reshape(1, width), row_owner)
+        compiler_params=ROOM,
+    )(in_vmem(base), in_vmem(far), norm_gain.reshape(1, width), row_owner)
     arrived = exchange(outgoing.reshape(owners, tiles, HEAD))
-    arrived = arrived.reshape(owners, tiles // 2, 2, HEAD).transpose(0, 2, 1, 3)
     return (hidden, arrived.reshape(1, 1, owners, 2, width))
 
 

time: 162 us -> 156 us (0.963)
  Pallas kernels: 27.5 us -> 22.1 us
  local copies, waits for them, and re-layouts: 3.64 us -> 1.22 us
    pallas_call x1, Pallas kernels: 11.2 us -> 8.13 us  [on_device(): pl.pallas_call(attend_kernel, grid_spec=pltpu.PrefetchScalarGridSpec(num_...]
    pallas_call x2, Pallas kernels: 6.43 us -> 4.12 us  [the longest x1 2.29 us: on_device(): pl.pallas_call(prep_kernel, grid=(1,), in_specs=[whole(x) for x in (queri...]
  transfers between devices with their start and end apart: 6 -> 6, of which waited for: 5 -> 5; matrix products, arithmetic and copies ran while one was open for 2% -> 3% of each run, Pallas kernels for 3% -> 3%
where the time goes in v3:
time: 156 us
  blocking collectives  56.5 us (36%)
  waiting for transfers between devices  42.7 us (27%)
  starting transfers between devices  27.6 us (18%)
  Pallas kernels  22.1 us (14%)
  other arithmetic  5.02 us (3%)
    all_to_all x2, blocking collectives, exchange(): return lax.all_to_all(x, 'wide', 0, 0, tiled=True, axis_index_groups=groups)  56.5 us
    all_to_all x2, starting transfers between devices, exchange(): return lax.all_to_all(x, 'wide', 0, 0, tiled=True, axis_index_groups=groups)  18.9 us
    all_to_all x2, waiting for transfers between devices, exchange(): return lax.all_to_all(x, 'wide', 0, 0, tiled=True, axis_index_groups=groups)  17.8 us
    ppermute x1, waiting for transfers between devices, on_device(): far = lax.ppermute(pair, 'narrow', [(2, 0), (3, 1)])  13.2 us
    pallas_call x2, Pallas kernels, project(): pl.pallas_call(projector(make_rows), grid_spec=pltpu.PrefetchScalarGridSp...  9.84 us
    ppermute x1, waiting for transfers between devices, on_device(): far_short = lax.ppermute(pair_short, 'narrow', [(0, 2), (1, 3)])  9.67 us
    pallas_call x1, Pallas kernels, on_device(): pl.pallas_call(attend_kernel, grid_spec=pltpu.PrefetchScalarGridSpec(num_...  8.13 us
    ppermute x1, starting transfers between devices, on_device(): far_short = lax.ppermute(pair_short, 'narrow', [(0, 2), (1, 3)])  3.46 us
  transfers between devices with their start and end apart: 6, of which 5 were waited for; matrix products, arithmetic and copies ran while one was open for 3% of the time, Pallas kernels for 3%

profile of v3, /device:TPU:32, one launch (start us, length us, event | category | flops | bytes accessed | tf_op | source)
XLA Modules:
  0.0 155.8 jit_solution(13910786318933859860)
XLA Ops:
  0.6 2.3 %prep.1 = (bf16[16,128,256]{2,1,0:T(8,128)(2,1)}, bf16[4,128,512]{2,1,0:T(8,128)(2,1)}) custom-call(bf16[256,512]{1,0:T(8,128)(2,1)} %refs_0_.1, bf16[256,128]{1,0:T(8,128)(2,1)} %refs_1_.2, bf16[256,128]{1,0:T(8,128)(2,1)} %refs_2_.1), custom_call_target="tpu_custom_call" | custom-call | tf_op jit(solution)/shard_map/prep/pallas_call | solution.py:282
  2.9 3.9 %all-to-all-start = ((bf16[4,128,512]{2,1,0:T(8,128)(2,1)}), bf16[4,128,512]{2,1,0:T(8,128)(2,1)S(1)}, u32[]{:S(2)}, u32[]{:S(2)}) async-start(bf16[4,128,512]{2,1,0:T(8,128)(2,1)} %get-tuple-element.24), calls=%async_computation | async-start | bytes 1048576 | tf_op jit(solution)/shard_map/all_to_all | solution.py:268
  6.8 5.1 %short.1 = (bf16[64,4096]{1,0:T(8,128)(2,1)}, bf16[64,4096]{1,0:T(8,128)(2,1)}) custom-call(s32[1]{0:T(128)} %bitcast.core_ref, bf16[256,512]{1,0:T(8,128)(2,1)} %refs_0_.1, bf16[256,128]{1,0:T(8,128)(2,1)} %refs_1_.2, bf16[256,128]{1,0:T(8,128)(2,1)} %refs_2_.1, s32[1,128]{1,0:T(1,128)} %refs_3_.1, bf16[512,4096]{1,0:T(8,128)(2,1)} %refs_1_.3), custom_call_target="tpu_custom_call" | custom-call | tf_op jit(solution)/shard_map/short/pallas_call | solution.py:216
  11.9 2.0 %collective-permute-start = (bf16[64,4096]{1,0:T(8,128)(2,1)}, bf16[64,4096]{1,0:T(8,128)(2,1)S(1)}, u32[]{:S(2)}, u32[]{:S(2)}) collective-permute-start(bf16[64,4096]{1,0:T(8,128)(2,1)} %get-tuple-element.22), channel_id=1, source_target_pairs={{0,4},{4,0},{8,12},{12,8},{1,5},{5,1},{9,13},{13,9},{2,6},{6,2},{1... | collective-permute-start | bytes 1572872 | tf_op jit(solution)/shard_map/ppermute | solution.py:304
  14.0 0.9 all-to-all-done.q_ref
  14.8 15.0 %all-to-all-start.1 = ((bf16[16,128,256]{2,1,0:T(8,128)(2,1)}), bf16[16,128,256]{2,1,0:T(8,128)(2,1)S(1)}, u32[]{:S(2)}, u32[]{:S(2)}) async-start(bf16[16,128,256]{2,1,0:T(8,128)(2,1)} %get-tuple-element.25), calls=%async_computation.1 | async-start | bytes 2097152 | tf_op jit(solution)/shard_map/all_to_all | solution.py:268
  29.8 1.2 fusion
  31.0 3.5 %collective-permute-start.1 = (bf16[64,4096]{1,0:T(8,128)(2,1)S(1)}, bf16[64,4096]{1,0:T(8,128)(2,1)}, u32[]{:S(2)}, u32[]{:S(2)}) collective-permute-start(bf16[64,4096]{1,0:T(8,128)(2,1)S(1)} %fusion), channel_id=1, source_target_pairs={{0,8},{4,12},{1,9},{5,13},{2,10},{6,14},{3,11},{7,15},{16,24},{20,... | collective-permute-start | bytes 1572872 | tf_op jit(solution)/shard_map/ppermute | solution.py:306
  34.4 9.7 %collective-permute-done.1 = bf16[64,4096]{1,0:T(8,128)(2,1)} collective-permute-done((bf16[64,4096]{1,0:T(8,128)(2,1)S(1)}, bf16[64,4096]{1,0:T(8,128)(2,1)}, u32[]{:S(2)}, u32[]{:S(2)}) %collective-permute-start.1) | collective-permute-done | bytes 524320 | tf_op jit(solution)/shard_map/ppermute | solution.py:306
  44.1 1.4 convert_add_fusion
  45.5 17.0 %all-to-all-done.1.kv_ref = bf16[16,128,256]{2,1,0:T(8,128)(2,1)S(1)} async-done(((bf16[16,128,256]{2,1,0:T(8,128)(2,1)}), bf16[16,128,256]{2,1,0:T(8,128)(2,1)S(1)}, u32[]{:S(2)}, u32[]{:S(2)}) %all-to-all-start.1) | async-done | bytes 1048608 | tf_op jit(solution)/shard_map/all_to_all | solution.py:268
  62.5 8.1 %attend.1 = bf16[4,144,512]{2,1,0:T(8,128)(2,1)S(1)} custom-call(s32[1]{0:T(128)} %bitcast.1.wide_ref, s32[64]{0:T(128)S(1)} %copy-done, bf16[4,128,512]{2,1,0:T(8,128)(2,1)S(1)} %all-to-all-done.q_ref, bf16[16,128,256]{2,1,0:T(8,128)(2,1)S(1)} %all-to-all-done.1.kv_ref), custom_call_target="tpu_custom_call" | custom-call | tf_op jit(solution)/shard_map/attend/pallas_call | solution.py:311
  70.6 14.7 %all_to_all.20.refs_0_ = bf16[4,144,512]{2,1,0:T(8,128)(2,1)S(1)} all-to-all(bf16[4,144,512]{2,1,0:T(8,128)(2,1)S(1)} %attend.1), channel_id=1, replica_groups={{0,16,128,144},{32,48,160,176},{64,80,192,208},{96,112,224,240},{256,27..., dimensions={0} | all-to-all | bytes 1179648 | tf_op jit(solution)/shard_map/all_to_all | solution.py:268
  85.4 4.7 %long.1 = (bf16[64,4096]{1,0:T(8,128)(2,1)}, bf16[64,4096]{1,0:T(8,128)(2,1)}) custom-call(s32[1]{0:T(128)} %bitcast.core_ref, bf16[4,144,512]{2,1,0:T(8,128)(2,1)S(1)} %all_to_all.20.refs_0_, bf16[512,4096]{1,0:T(8,128)(2,1)} %refs_1_.3), custom_call_target="tpu_custom_call" | custom-call | tf_op jit(solution)/shard_map/long/pallas_call | solution.py:216
  90.1 1.9 %collective-permute-start.2 = (bf16[64,4096]{1,0:T(8,128)(2,1)}, bf16[64,4096]{1,0:T(8,128)(2,1)S(1)}, u32[]{:S(2)}, u32[]{:S(2)}) collective-permute-start(bf16[64,4096]{1,0:T(8,128)(2,1)} %get-tuple-element.27), channel_id=1, source_target_pairs={{0,4},{4,0},{8,12},{12,8},{1,5},{5,1},{9,13},{13,9},{2,6},{6,2},{1... | collective-permute-start | bytes 1572872 | tf_op jit(solution)/shard_map/ppermute | solution.py:331
  92.0 0.1 copy.11.owner_ref
  92.1 2.0 %collective-permute-done.2 = bf16[64,4096]{1,0:T(8,128)(2,1)S(1)} collective-permute-done((bf16[64,4096]{1,0:T(8,128)(2,1)}, bf16[64,4096]{1,0:T(8,128)(2,1)S(1)}, u32[]{:S(2)}, u32[]{:S(2)}) %collective-permute-start.2) | collective-permute-done | bytes 524320 | tf_op jit(solution)/shard_map/ppermute | solution.py:331
  94.1 1.2 add_convert_fusion
  95.3 1.3 collective-permute-start.3
  96.6 1.3 select_add_fusion.base_ref
  97.9 13.2 %collective-permute-done.3.far_ref = bf16[64,4096]{1,0:T(8,128)(2,1)S(1)} collective-permute-done((bf16[64,4096]{1,0:T(8,128)(2,1)S(1)}, bf16[64,4096]{1,0:T(8,128)(2,1)S(1)}, u32[]{:S(2)}, u32[]{:S(2)}) %collective-permute-start.3) | collective-permute-done | bytes 524320 | tf_op jit(solution)/shard_map/ppermute | solution.py:333
  111.1 1.8 %route.1 = (bf16[64,4096]{1,0:T(8,128)(2,1)}, bf16[4096,128]{1,0:T(8,128)(2,1)S(1)}) custom-call(f32[64,4096]{1,0:T(8,128)S(1)} %select_add_fusion.base_ref, bf16[64,4096]{1,0:T(8,128)(2,1)S(1)} %collective-permute-done.3.far_ref, bf16[1,4096]{1,0:T(2,128)(2,1)S(1)} %reshape.27.gain_ref, s32[64,1]{1,0:T(8,128)S(1)} %copy.11.owner_ref), custom_call_target="tpu_custom_call" | custom-call | tf_op jit(solution)/shard_map/route/pallas_call | solution.py:339
  113.0 41.7 %all_to_all.21 = bf16[64,64,128]{2,1,0:T(8,128)(2,1)S(1)} all-to-all(bf16[64,64,128]{2,1,0:T(8,128)(2,1)S(1)} %bitcast.3), channel_id=1, replica_groups=mesh['wide'=64,'narrow'=4,'rep'=4] {'wide'}, dimensions={0} | all-to-all | bytes 2097152 | tf_op jit(solution)/shard_map/all_to_all | solution.py:268
  154.7 1.1 reshape.29
  (10 shorter events, 0.0 us)
Async XLA Ops:
  2.9 11.9 %all-to-all-start = ((bf16[4,128,512]{2,1,0:T(8,128)(2,1)}), bf16[4,128,512]{2,1,0:T(8,128)(2,1)S(1)}, u32[]{:S(2)}, u32[]{:S(2)}) async-start(bf16[4,128,512]{2,1,0:T(8,128)(2,1)} %get-tuple-element.24), calls=%async_computation | async-start | bytes 1048576 | tf_op jit(solution)/shard_map/all_to_all | solution.py:268
  11.9 50.6 %copy-start = (s32[64]{0:T(128)S(1)}, s32[64]{0:T(128)}, u32[]{:S(2)}) copy-start(s32[64]{0:T(128)} %span_ref.1) | copy-start | bytes 772
  11.9 17.9 %collective-permute-start = (bf16[64,4096]{1,0:T(8,128)(2,1)}, bf16[64,4096]{1,0:T(8,128)(2,1)S(1)}, u32[]{:S(2)}, u32[]{:S(2)}) collective-permute-start(bf16[64,4096]{1,0:T(8,128)(2,1)} %get-tuple-element.22), channel_id=1, source_target_pairs={{0,4},{4,0},{8,12},{12,8},{1,5},{5,1},{9,13},{13,9},{2,6},{6,2},{1... | collective-permute-start | bytes 1572872 | tf_op jit(solution)/shard_map/ppermute | solution.py:304
  14.8 47.6 %all-to-all-start.1 = ((bf16[16,128,256]{2,1,0:T(8,128)(2,1)}), bf16[16,128,256]{2,1,0:T(8,128)(2,1)S(1)}, u32[]{:S(2)}, u32[]{:S(2)}) async-start(bf16[16,128,256]{2,1,0:T(8,128)(2,1)} %get-tuple-element.25), calls=%async_computation.1 | async-start | bytes 2097152 | tf_op jit(solution)/shard_map/all_to_all | solution.py:268
  31.0 13.1 %collective-permute-start.1 = (bf16[64,4096]{1,0:T(8,128)(2,1)S(1)}, bf16[64,4096]{1,0:T(8,128)(2,1)}, u32[]{:S(2)}, u32[]{:S(2)}) collective-permute-start(bf16[64,4096]{1,0:T(8,128)(2,1)S(1)} %fusion), channel_id=1, source_target_pairs={{0,8},{4,12},{1,9},{5,13},{2,10},{6,14},{3,11},{7,15},{16,24},{20,... | collective-permute-start | bytes 1572872 | tf_op jit(solution)/shard_map/ppermute | solution.py:306
  45.5 46.5 %copy-start.3 = (s32[64,1]{0,1:T(1,128)S(1)}, s32[64,1]{0,1:T(1,128)}, u32[]{:S(2)}) copy-start(s32[64,1]{0,1:T(1,128)} %param.17) | copy-start | bytes 772
  45.5 46.6 %copy-start.2 = (bf16[4096]{0:T(1024)(128)(2,1)S(1)}, bf16[4096]{0:T(1024)(128)(2,1)}, u32[]{:S(2)}) copy-start(bf16[4096]{0:T(1024)(128)(2,1)} %param.14) | copy-start | bytes 24580
  70.6 26.0 %copy-start.1 = (bf16[64,4096]{1,0:T(8,128)(2,1)S(1)}, bf16[64,4096]{1,0:T(8,128)(2,1)}, u32[]{:S(2)}) copy-start(bf16[64,4096]{1,0:T(8,128)(2,1)} %param.12) | copy-start | bytes 1572868
  90.1 4.0 %collective-permute-start.2 = (bf16[64,4096]{1,0:T(8,128)(2,1)}, bf16[64,4096]{1,0:T(8,128)(2,1)S(1)}, u32[]{:S(2)}, u32[]{:S(2)}) collective-permute-start(bf16[64,4096]{1,0:T(8,128)(2,1)} %get-tuple-element.27), channel_id=1, source_target_pairs={{0,4},{4,0},{8,12},{12,8},{1,5},{5,1},{9,13},{13,9},{2,6},{6,2},{1... | collective-permute-start | bytes 1572872 | tf_op jit(solution)/shard_map/ppermute | solution.py:331
  95.3 15.9 %collective-permute-start.3 = (bf16[64,4096]{1,0:T(8,128)(2,1)S(1)}, bf16[64,4096]{1,0:T(8,128)(2,1)S(1)}, u32[]{:S(2)}, u32[]{:S(2)}) collective-permute-start(bf16[64,4096]{1,0:T(8,128)(2,1)S(1)} %add_convert_fusion), channel_id=1, source_target_pairs={{8,0},{12,4},{9,1},{13,5},{10,2},{14,6},{11,3},{15,7},{24,16},{28,... | collective-permute-start | bytes 1572872 | tf_op jit(solution)/shard_map/ppermute | solution.py:333

commit v4 on v3

--- a/solution.py
+++ b/solution.py
@@ -13,6 +13,7 @@
 FAR = -1e30
 ROOM = pltpu.CompilerParams(vmem_limit_bytes=24 * 1024 * 1024)
 STATS = 16
+FLIPS = (1, SIDE, SIDE + 1)
 STEP = 4
 SCALE2 = SCALE * 1.4426950408889634
 QUERY_GROUPS = [
@@ -53,9 +54,7 @@
     kv = jnp.concatenate([k_ref[:LONG_DEV], v_ref[:LONG_DEV].T], axis=1)
     for i in range(kv_out.shape[0]):
         kv_out[i] = kv
-    q = heads_across(q_ref[:LONG_DEV])
-    for j in range(q_out.shape[0]):
-        q_out[j] = q
+    q_out[...] = heads_across(q_ref[:LONG_DEV])
 
 
 def short_rows(q_ref, k_ref, v_ref, seg_ref):
@@ -85,15 +84,38 @@
     return high, middle, rest - middle
 
 
+def member(w):
+    return (w // SIDE % 2) * 2 + w % 2
+
+
 def attend_kernel(
-    wide_ref, span_ref, q_ref, kv_ref, out_ref, list_ref, top_ref, sum_ref, acc_ref
+    wide_ref,
+    span_ref,
+    q0_ref,
+    q1_ref,
+    q2_ref,
+    q3_ref,
+    kv_ref,
+    out_ref,
+    list_ref,
+    q_ref,
+    top_ref,
+    sum_ref,
+    acc_ref,
 ):
-    j = pl.program_id(0)
+    r = pl.program_id(0)
     w = wide_ref[0]
     y = w // SIDE
     x = w % SIDE
+    j = r ^ member(w)
+
+    @pl.when(r == 0)
+    def _():
+        for i, ref in enumerate((q0_ref, q1_ref, q2_ref, q3_ref)):
+            q_ref[i] = ref[...]
+
     q_span = span_ref[((y // 2) * 2 + j // 2) * SIDE + (x // 2) * 2 + j % 2]
-    qs = q_ref[j]
+    qs = q_ref[r]
     cols = qs.shape[1]
     half = cols // 2
     count = jnp.int32(0)
@@ -103,7 +125,7 @@
         count = count + jnp.where(span < q_span, 1, 0)
     for i in range(STEP):
         list_ref[count + i] = 0
-    own = j == (y % 2) * 2 + x % 2
+    own = r == 0
 
     @pl.when(own)
     def _():
@@ -207,7 +229,7 @@
     return pl.BlockSpec(x.shape, lambda *i: (0,) * x.ndim)
 
 
-def project(make_rows, core, inputs, specs, weight, name):
+def project(make_rows, core, inputs, specs, weight):
     cols, width = weight.shape
     half = LONG_DEV // 2
     block = 1024
@@ -226,7 +248,6 @@
             scratch_shapes=[pltpu.VMEM((2 * half, cols), jnp.bfloat16)],
         ),
         out_shape=(shape, shape),
-        name=name,
     )(core, *inputs, weight)
 
 
@@ -285,21 +306,24 @@
         in_specs=[whole(x) for x in (queries, key_rows, value_rows)],
         out_specs=(
             pl.BlockSpec((16, LONG_DEV, 2 * HEAD), lambda i: (0, 0, 0)),
-            pl.BlockSpec((4, LONG_DEV, cols), lambda i: (0, 0, 0)),
+            pl.BlockSpec((LONG_DEV, cols), lambda i: (0, 0)),
         ),
         out_shape=(
             jax.ShapeDtypeStruct((16, LONG_DEV, 2 * HEAD), bf),
-            jax.ShapeDtypeStruct((4, LONG_DEV, cols), bf),
+            jax.ShapeDtypeStruct((LONG_DEV, cols), bf),
         ),
         name="prep",
     )(queries, key_rows, value_rows)
     across = [(0, 1), (1, 0), (2, 3), (3, 2)]
     kv, qs, core_after = lax.optimization_barrier((kv, qs, core))
     kv = exchange(kv, KEY_GROUPS)
-    qs = exchange(qs, QUERY_GROUPS)
+    devices = range(SIDE * SIDE)
+    queries_by = [qs] + [
+        lax.ppermute(qs, "wide", [(i, i ^ flip) for i in devices]) for flip in FLIPS
+    ]
     short_in = (queries, key_rows, value_rows, segments)
     send, keep_short = project(
-        short_rows, core_after, short_in, [whole(x) for x in short_in], out_weight, "short"
+        short_rows, core_after, short_in, [whole(x) for x in short_in], out_weight
     )
     near_short = lax.ppermute(send, "narrow", across)
     pair_short = pair_sum(keep_short, near_short)
@@ -313,10 +337,13 @@
         grid_spec=pltpu.PrefetchScalarGridSpec(
             num_scalar_prefetch=2,
             grid=(4,),
-            in_specs=[vmem, vmem],
-            out_specs=pl.BlockSpec((1, HEAD + STATS, cols), lambda j, w, m: (j, 0, 0)),
+            in_specs=[vmem] * 5,
+            out_specs=pl.BlockSpec(
+                (1, HEAD + STATS, cols), lambda r, w, m: (r ^ member(w[0]), 0, 0)
+            ),
             scratch_shapes=[
                 pltpu.SMEM((16 + STEP,), jnp.int32),
+                pltpu.VMEM((4, LONG_DEV, cols), bf),
                 pltpu.VMEM((1, cols), jnp.float32),
                 pltpu.VMEM((1, cols), jnp.float32),
                 pltpu.VMEM((HEAD, cols), jnp.float32),
@@ -325,9 +352,9 @@
         out_shape=jax.ShapeDtypeStruct((4, HEAD + STATS, cols), bf),
         name="attend",
         compiler_params=ROOM,
-    )(wide, span_map, in_vmem(qs), in_vmem(kv))
+    )(wide, span_map, *map(in_vmem, queries_by), in_vmem(kv))
     got = exchange(parts, QUERY_GROUPS)
-    send, keep = project(merged_rows, core, (in_vmem(got),), [vmem], out_weight, "long")
+    send, keep = project(merged_rows, core, (in_vmem(got),), [vmem], out_weight)
     near = lax.ppermute(send, "narrow", across)
     pair, keep, near = lax.optimization_barrier((pair_sum(keep, near), keep, near))
     far = lax.ppermute(pair, "narrow", [(2, 0), (3, 1)])

time: 156 us -> 154 us (0.987)
  waiting for transfers between devices: 42.7 us -> 35.9 us
  starting transfers between devices: 27.6 us -> 33 us
    all_to_all x2 -> x1, waiting for transfers between devices: 17.8 us -> 0.7 us  [exchange(): return lax.all_to_all(x, 'wide', 0, 0, tiled=True, axis_index_groups=groups)]
    ppermute x0 -> x3, waiting for transfers between devices: none -> 15.2 us  [on_device(): lax.ppermute(qs, 'wide', [(i, i ^ flip) for i in devices])]
    ppermute x0 -> x3, starting transfers between devices: none -> 9.2 us  [on_device(): lax.ppermute(qs, 'wide', [(i, i ^ flip) for i in devices])]
    ppermute x1, waiting for transfers between devices: 9.67 us -> 1.49 us  [on_device(): far_short = lax.ppermute(pair_short, 'narrow', [(0, 2), (1, 3)])]
    ppermute x1, waiting for transfers between devices: 13.2 us -> 16.5 us  [on_device(): far = lax.ppermute(pair, 'narrow', [(2, 0), (3, 1)])]
    all_to_all x2 -> x1, starting transfers between devices: 18.9 us -> 16.2 us  [exchange(): return lax.all_to_all(x, 'wide', 0, 0, tiled=True, axis_index_groups=groups)]
  transfers between devices with their start and end apart: 6 -> 8, of which waited for: 5 -> 6; matrix products, arithmetic and copies ran while one was open for 3% -> 3% of each run, Pallas kernels for 3% -> 0%
where the time goes in v4:
time: 154 us; the launch traced here: 153 us
  blocking collectives  55 us (36%)
  waiting for transfers between devices  35.9 us (23%)
  starting transfers between devices  33 us (21%)
  Pallas kernels  22 us (14%)
  other arithmetic  5.01 us (3%)
    all_to_all x2, blocking collectives, exchange(): return lax.all_to_all(x, 'wide', 0, 0, tiled=True, axis_index_groups=groups)  55 us
    ppermute x1, waiting for transfers between devices, on_device(): far = lax.ppermute(pair, 'narrow', [(2, 0), (3, 1)])  16.5 us
    all_to_all x1, starting transfers between devices, exchange(): return lax.all_to_all(x, 'wide', 0, 0, tiled=True, axis_index_groups=groups)  16.2 us
    ppermute x3, waiting for transfers between devices, on_device(): lax.ppermute(qs, 'wide', [(i, i ^ flip) for i in devices])  15.2 us
    pallas_call x2, Pallas kernels, project(): pl.pallas_call(projector(make_rows), grid_spec=pltpu.PrefetchScalarGridSp...  9.9 us
    ppermute x3, starting transfers between devices, on_device(): lax.ppermute(qs, 'wide', [(i, i ^ flip) for i in devices])  9.2 us
    pallas_call x1, Pallas kernels, on_device(): pl.pallas_call(attend_kernel, grid_spec=pltpu.PrefetchScalarGridSpec(num_...  8.12 us
  transfers between devices with their start and end apart: 8, of which 6 were waited for; matrix products, arithmetic and copies ran while one was open for 3% of the time, Pallas kernels for 0%

profile of v4, /device:TPU:32, one launch (start us, length us, event | category | flops | bytes accessed | tf_op | source)
XLA Modules:
  0.0 153.0 jit_solution(18207121874401198516)
XLA Ops:
  0.6 2.1 %prep.1 = (bf16[16,128,256]{2,1,0:T(8,128)(2,1)}, bf16[128,512]{1,0:T(8,128)(2,1)}) custom-call(bf16[256,512]{1,0:T(8,128)(2,1)} %refs_0_.1, bf16[256,128]{1,0:T(8,128)(2,1)} %refs_1_.2, bf16[256,128]{1,0:T(8,128)(2,1)} %refs_2_.1), custom_call_target="tpu_custom_call" | custom-call | tf_op jit(solution)/shard_map/prep/pallas_call | solution.py:303
  2.8 5.2 %shard_map.104 = (bf16[64,4096]{1,0:T(8,128)(2,1)}, bf16[64,4096]{1,0:T(8,128)(2,1)}) custom-call(s32[1]{0:T(128)} %bitcast.core_ref, bf16[256,512]{1,0:T(8,128)(2,1)} %refs_0_.1, bf16[256,128]{1,0:T(8,128)(2,1)} %refs_1_.2, bf16[256,128]{1,0:T(8,128)(2,1)} %refs_2_.1, s32[1,128]{1,0:T(1,128)} %refs_3_.1, bf16[512,4096]{1,0:T(8,128)(2,1)} %refs_1_.3), custom_call_target="tpu_custom_call" | custom-call | tf_op jit(solution)/shard_map/pallas_call | solution.py:238
  8.0 2.0 %collective-permute-start = (bf16[64,4096]{1,0:T(8,128)(2,1)}, bf16[64,4096]{1,0:T(8,128)(2,1)S(1)}, u32[]{:S(2)}, u32[]{:S(2)}) collective-permute-start(bf16[64,4096]{1,0:T(8,128)(2,1)} %get-tuple-element.22), channel_id=1, source_target_pairs={{0,4},{4,0},{8,12},{12,8},{1,5},{5,1},{9,13},{13,9},{2,6},{6,2},{1... | collective-permute-start | bytes 1572872 | tf_op jit(solution)/shard_map/ppermute | solution.py:328
  10.0 16.2 %all-to-all-start = ((bf16[16,128,256]{2,1,0:T(8,128)(2,1)}), bf16[16,128,256]{2,1,0:T(8,128)(2,1)S(1)}, u32[]{:S(2)}, u32[]{:S(2)}) async-start(bf16[16,128,256]{2,1,0:T(8,128)(2,1)} %get-tuple-element.25), calls=%async_computation | async-start | bytes 2097152 | tf_op jit(solution)/shard_map/all_to_all | solution.py:289
  26.2 1.2 fusion
  27.4 2.4 %collective-permute-start.1 = (bf16[64,4096]{1,0:T(8,128)(2,1)S(1)}, bf16[64,4096]{1,0:T(8,128)(2,1)}, u32[]{:S(2)}, u32[]{:S(2)}) collective-permute-start(bf16[64,4096]{1,0:T(8,128)(2,1)S(1)} %fusion), channel_id=1, source_target_pairs={{0,8},{4,12},{1,9},{5,13},{2,10},{6,14},{3,11},{7,15},{16,24},{20,... | collective-permute-start | bytes 1572872 | tf_op jit(solution)/shard_map/ppermute | solution.py:330
  29.8 2.5 %collective-permute-start.2 = (bf16[128,512]{1,0:T(8,128)(2,1)S(1)}, bf16[128,512]{1,0:T(8,128)(2,1)S(1)}, u32[]{:S(2)}, u32[]{:S(2)}) collective-permute-start(bf16[128,512]{1,0:T(8,128)(2,1)S(1)} %copy-done), channel_id=1, source_target_pairs={{0,16},{16,0},{32,48},{48,32},{64,80},{80,64},{96,112},{112,96},{1... | collective-permute-start | bytes 393224 | tf_op jit(solution)/shard_map/ppermute | solution.py:322
  32.3 2.7 %collective-permute-start.3 = (bf16[128,512]{1,0:T(8,128)(2,1)S(1)}, bf16[128,512]{1,0:T(8,128)(2,1)S(1)}, u32[]{:S(2)}, u32[]{:S(2)}) collective-permute-start(bf16[128,512]{1,0:T(8,128)(2,1)S(1)} %copy-done), channel_id=1, source_target_pairs={{0,128},{16,144},{32,160},{48,176},{64,192},{80,208},{96,224},{112... | collective-permute-start | bytes 393224 | tf_op jit(solution)/shard_map/ppermute | solution.py:322
  35.0 4.0 %collective-permute-start.4 = (bf16[128,512]{1,0:T(8,128)(2,1)S(1)}, bf16[128,512]{1,0:T(8,128)(2,1)S(1)}, u32[]{:S(2)}, u32[]{:S(2)}) collective-permute-start(bf16[128,512]{1,0:T(8,128)(2,1)S(1)} %copy-done), channel_id=1, source_target_pairs={{0,144},{16,128},{32,176},{48,160},{64,208},{80,192},{96,240},{112... | collective-permute-start | bytes 393224 | tf_op jit(solution)/shard_map/ppermute | solution.py:322
  39.0 1.5 collective-permute-done.1
  40.5 1.4 convert_add_fusion
  41.9 12.4 %collective-permute-done.2.q1_ref = bf16[128,512]{1,0:T(8,128)(2,1)S(1)} collective-permute-done((bf16[128,512]{1,0:T(8,128)(2,1)S(1)}, bf16[128,512]{1,0:T(8,128)(2,1)S(1)}, u32[]{:S(2)}, u32[]{:S(2)}) %collective-permute-start.2) | collective-permute-done | bytes 131104 | tf_op jit(solution)/shard_map/ppermute | solution.py:322
  54.4 2.8 %collective-permute-done.4.q3_ref = bf16[128,512]{1,0:T(8,128)(2,1)S(1)} collective-permute-done((bf16[128,512]{1,0:T(8,128)(2,1)S(1)}, bf16[128,512]{1,0:T(8,128)(2,1)S(1)}, u32[]{:S(2)}, u32[]{:S(2)}) %collective-permute-start.4) | collective-permute-done | bytes 131104 | tf_op jit(solution)/shard_map/ppermute | solution.py:322
  57.8 8.1 %attend.1 = bf16[4,144,512]{2,1,0:T(8,128)(2,1)S(1)} custom-call(s32[1]{0:T(128)} %bitcast.1.wide_ref, s32[64]{0:T(128)S(1)} %copy-done.1, bf16[128,512]{1,0:T(8,128)(2,1)S(1)} %copy-done, bf16[128,512]{1,0:T(8,128)(2,1)S(1)} %collective-permute-done.2.q1_ref, bf16[128,512]{1,0:T(8,128)(2,1)S(1)} %collective-permute-done.3.q2_ref, ...), custom_call_target="tpu_custom_call" | custom-call | tf_op jit(solution)/shard_map/attend/pallas_call | solution.py:335
  66.0 12.2 %all_to_all.15.refs_0_ = bf16[4,144,512]{2,1,0:T(8,128)(2,1)S(1)} all-to-all(bf16[4,144,512]{2,1,0:T(8,128)(2,1)S(1)} %attend.1), channel_id=1, replica_groups={{0,16,128,144},{32,48,160,176},{64,80,192,208},{96,112,224,240},{256,27..., dimensions={0} | all-to-all | bytes 1179648 | tf_op jit(solution)/shard_map/all_to_all | solution.py:289
  78.2 4.7 %shard_map.105 = (bf16[64,4096]{1,0:T(8,128)(2,1)}, bf16[64,4096]{1,0:T(8,128)(2,1)}) custom-call(s32[1]{0:T(128)} %bitcast.core_ref, bf16[4,144,512]{2,1,0:T(8,128)(2,1)S(1)} %all_to_all.15.refs_0_, bf16[512,4096]{1,0:T(8,128)(2,1)} %refs_1_.3), custom_call_target="tpu_custom_call" | custom-call | tf_op jit(solution)/shard_map/pallas_call | solution.py:238
  82.9 1.9 %collective-permute-start.5 = (bf16[64,4096]{1,0:T(8,128)(2,1)}, bf16[64,4096]{1,0:T(8,128)(2,1)S(1)}, u32[]{:S(2)}, u32[]{:S(2)}) collective-permute-start(bf16[64,4096]{1,0:T(8,128)(2,1)} %get-tuple-element.27), channel_id=1, source_target_pairs={{0,4},{4,0},{8,12},{12,8},{1,5},{5,1},{9,13},{13,9},{2,6},{6,2},{1... | collective-permute-start | bytes 1572872 | tf_op jit(solution)/shard_map/ppermute | solution.py:358
  85.0 2.0 %collective-permute-done.5 = bf16[64,4096]{1,0:T(8,128)(2,1)S(1)} collective-permute-done((bf16[64,4096]{1,0:T(8,128)(2,1)}, bf16[64,4096]{1,0:T(8,128)(2,1)S(1)}, u32[]{:S(2)}, u32[]{:S(2)}) %collective-permute-start.5) | collective-permute-done | bytes 524320 | tf_op jit(solution)/shard_map/ppermute | solution.py:358
  86.9 1.2 add_convert_fusion
  88.1 1.3 collective-permute-start.6
  89.4 1.3 select_add_fusion.base_ref
  90.7 16.5 %collective-permute-done.6.far_ref = bf16[64,4096]{1,0:T(8,128)(2,1)S(1)} collective-permute-done((bf16[64,4096]{1,0:T(8,128)(2,1)S(1)}, bf16[64,4096]{1,0:T(8,128)(2,1)S(1)}, u32[]{:S(2)}, u32[]{:S(2)}) %collective-permute-start.6) | collective-permute-done | bytes 524320 | tf_op jit(solution)/shard_map/ppermute | solution.py:360
  107.2 1.8 %route.1 = (bf16[64,4096]{1,0:T(8,128)(2,1)}, bf16[4096,128]{1,0:T(8,128)(2,1)S(1)}) custom-call(f32[64,4096]{1,0:T(8,128)S(1)} %select_add_fusion.base_ref, bf16[64,4096]{1,0:T(8,128)(2,1)S(1)} %collective-permute-done.6.far_ref, bf16[1,4096]{1,0:T(2,128)(2,1)S(1)} %reshape.27.gain_ref, s32[64,1]{1,0:T(8,128)S(1)} %copy.11.owner_ref), custom_call_target="tpu_custom_call" | custom-call | tf_op jit(solution)/shard_map/route/pallas_call | solution.py:366
  109.1 42.8 %all_to_all.16 = bf16[64,64,128]{2,1,0:T(8,128)(2,1)S(1)} all-to-all(bf16[64,64,128]{2,1,0:T(8,128)(2,1)S(1)} %bitcast.3), channel_id=1, replica_groups=mesh['wide'=64,'narrow'=4,'rep'=4] {'wide'}, dimensions={0} | all-to-all | bytes 2097152 | tf_op jit(solution)/shard_map/all_to_all | solution.py:289
  (16 shorter events, 1.9 us)
Async XLA Ops:
  2.8 27.0 %copy-start = (bf16[128,512]{1,0:T(8,128)(2,1)S(1)}, bf16[128,512]{1,0:T(8,128)(2,1)}, u32[]{:S(2)}) copy-start(bf16[128,512]{1,0:T(8,128)(2,1)} %get-tuple-element.24.q0_ref) | copy-start | bytes 393220
  8.0 49.9 %copy-start.1 = (s32[64]{0:T(128)S(1)}, s32[64]{0:T(128)}, u32[]{:S(2)}) copy-start(s32[64]{0:T(128)} %span_ref.1) | copy-start | bytes 772
  8.0 18.3 %collective-permute-start = (bf16[64,4096]{1,0:T(8,128)(2,1)}, bf16[64,4096]{1,0:T(8,128)(2,1)S(1)}, u32[]{:S(2)}, u32[]{:S(2)}) collective-permute-start(bf16[64,4096]{1,0:T(8,128)(2,1)} %get-tuple-element.22), channel_id=1, source_target_pairs={{0,4},{4,0},{8,12},{12,8},{1,5},{5,1},{9,13},{13,9},{2,6},{6,2},{1... | collective-permute-start | bytes 1572872 | tf_op jit(solution)/shard_map/ppermute | solution.py:328
  10.0 47.8 %all-to-all-start = ((bf16[16,128,256]{2,1,0:T(8,128)(2,1)}), bf16[16,128,256]{2,1,0:T(8,128)(2,1)S(1)}, u32[]{:S(2)}, u32[]{:S(2)}) async-start(bf16[16,128,256]{2,1,0:T(8,128)(2,1)} %get-tuple-element.25), calls=%async_computation | async-start | bytes 2097152 | tf_op jit(solution)/shard_map/all_to_all | solution.py:289
  27.4 13.1 %collective-permute-start.1 = (bf16[64,4096]{1,0:T(8,128)(2,1)S(1)}, bf16[64,4096]{1,0:T(8,128)(2,1)}, u32[]{:S(2)}, u32[]{:S(2)}) collective-permute-start(bf16[64,4096]{1,0:T(8,128)(2,1)S(1)} %fusion), channel_id=1, source_target_pairs={{0,8},{4,12},{1,9},{5,13},{2,10},{6,14},{3,11},{7,15},{16,24},{20,... | collective-permute-start | bytes 1572872 | tf_op jit(solution)/shard_map/ppermute | solution.py:330
  29.8 24.6 %collective-permute-start.2 = (bf16[128,512]{1,0:T(8,128)(2,1)S(1)}, bf16[128,512]{1,0:T(8,128)(2,1)S(1)}, u32[]{:S(2)}, u32[]{:S(2)}) collective-permute-start(bf16[128,512]{1,0:T(8,128)(2,1)S(1)} %copy-done), channel_id=1, source_target_pairs={{0,16},{16,0},{32,48},{48,32},{64,80},{80,64},{96,112},{112,96},{1... | collective-permute-start | bytes 393224 | tf_op jit(solution)/shard_map/ppermute | solution.py:322
  32.3 22.1 %collective-permute-start.3 = (bf16[128,512]{1,0:T(8,128)(2,1)S(1)}, bf16[128,512]{1,0:T(8,128)(2,1)S(1)}, u32[]{:S(2)}, u32[]{:S(2)}) collective-permute-start(bf16[128,512]{1,0:T(8,128)(2,1)S(1)} %copy-done), channel_id=1, source_target_pairs={{0,128},{16,144},{32,160},{48,176},{64,192},{80,208},{96,224},{112... | collective-permute-start | bytes 393224 | tf_op jit(solution)/shard_map/ppermute | solution.py:322
  35.0 22.1 %collective-permute-start.4 = (bf16[128,512]{1,0:T(8,128)(2,1)S(1)}, bf16[128,512]{1,0:T(8,128)(2,1)S(1)}, u32[]{:S(2)}, u32[]{:S(2)}) collective-permute-start(bf16[128,512]{1,0:T(8,128)(2,1)S(1)} %copy-done), channel_id=1, source_target_pairs={{0,144},{16,128},{32,176},{48,160},{64,208},{80,192},{96,240},{112... | collective-permute-start | bytes 393224 | tf_op jit(solution)/shard_map/ppermute | solution.py:322
  41.9 42.9 %copy-start.4 = (s32[64,1]{0,1:T(1,128)S(1)}, s32[64,1]{0,1:T(1,128)}, u32[]{:S(2)}) copy-start(s32[64,1]{0,1:T(1,128)} %param.17) | copy-start | bytes 772
  41.9 43.0 %copy-start.3 = (bf16[4096]{0:T(1024)(128)(2,1)S(1)}, bf16[4096]{0:T(1024)(128)(2,1)}, u32[]{:S(2)}) copy-start(bf16[4096]{0:T(1024)(128)(2,1)} %param.14) | copy-start | bytes 24580
  66.0 23.4 %copy-start.2 = (bf16[64,4096]{1,0:T(8,128)(2,1)S(1)}, bf16[64,4096]{1,0:T(8,128)(2,1)}, u32[]{:S(2)}) copy-start(bf16[64,4096]{1,0:T(8,128)(2,1)} %param.12) | copy-start | bytes 1572868
  82.9 4.0 %collective-permute-start.5 = (bf16[64,4096]{1,0:T(8,128)(2,1)}, bf16[64,4096]{1,0:T(8,128)(2,1)S(1)}, u32[]{:S(2)}, u32[]{:S(2)}) collective-permute-start(bf16[64,4096]{1,0:T(8,128)(2,1)} %get-tuple-element.27), channel_id=1, source_target_pairs={{0,4},{4,0},{8,12},{12,8},{1,5},{5,1},{9,13},{13,9},{2,6},{6,2},{1... | collective-permute-start | bytes 1572872 | tf_op jit(solution)/shard_map/ppermute | solution.py:358
  88.1 19.1 %collective-permute-start.6 = (bf16[64,4096]{1,0:T(8,128)(2,1)S(1)}, bf16[64,4096]{1,0:T(8,128)(2,1)S(1)}, u32[]{:S(2)}, u32[]{:S(2)}) collective-permute-start(bf16[64,4096]{1,0:T(8,128)(2,1)S(1)} %add_convert_fusion), channel_id=1, source_target_pairs={{8,0},{12,4},{9,1},{13,5},{10,2},{14,6},{11,3},{15,7},{24,16},{28,... | collective-permute-start | bytes 1572872 | tf_op jit(solution)/shard_map/ppermute | solution.py:360

commit v5 on v4

--- a/solution.py
+++ b/solution.py
@@ -229,8 +229,9 @@
     return pl.BlockSpec(x.shape, lambda *i: (0,) * x.ndim)
 
 
-def project(make_rows, core, inputs, specs, weight):
+def project(make_rows, core, inputs, specs, weight, parts=1):
     cols, width = weight.shape
+    width = width // parts
     half = LONG_DEV // 2
     block = 1024
     out = pl.BlockSpec((half, block), lambda i, c: (0, i))
@@ -244,19 +245,54 @@
                 *specs,
                 pl.BlockSpec((cols, block), lambda i, c: (0, i)),
             ],
-            out_specs=[out, out],
-            scratch_shapes=[pltpu.VMEM((2 * half, cols), jnp.bfloat16)],
-        ),
+            out_specs=[out, out, pl.BlockSpec((2 * half, cols), lambda i, c: (0, 0))],
+        ),
+        out_shape=(shape, shape, jax.ShapeDtypeStruct((2 * half, cols), jnp.bfloat16)),
+    )(core, *inputs, weight)
+
+
+def rest_kernel(rows_ref, weight_ref, send_ref, keep_ref):
+    rounded = dot(rows_ref[...], weight_ref[...]).astype(jnp.bfloat16)
+    half = send_ref.shape[0]
+    send_ref[...] = rounded[:half]
+    keep_ref[...] = rounded[half:]
+
+
+def project_rest(rows, weight):
+    cols, width = weight.shape
+    width = width // 2
+    half = LONG_DEV // 2
+    block = 1024
+    first = width // block
+    out = pl.BlockSpec((half, block), lambda i: (0, i))
+    shape = jax.ShapeDtypeStruct((half, width), jnp.bfloat16)
+    return pl.pallas_call(
+        rest_kernel,
+        grid=(width // block,),
+        in_specs=[
+            pl.BlockSpec((2 * half, cols), lambda i: (0, 0)),
+            pl.BlockSpec((cols, block), lambda i: (0, i + first)),
+        ],
+        out_specs=[out, out],
         out_shape=(shape, shape),
-    )(core, *inputs, weight)
+        name="rest",
+    )(rows, weight)
 
 
 def pair_sum(a, b):
     return (a.astype(jnp.float32) + b.astype(jnp.float32)).astype(jnp.bfloat16)
 
 
-def route_kernel(base_ref, far_ref, gain_ref, owner_ref, hidden_ref, out_ref, wide_ref):
-    hidden = (base_ref[...] + far_ref[...].astype(jnp.float32)).astype(jnp.bfloat16)
+def route_kernel(
+    base0_ref, base1_ref, far0_ref, far1_ref, gain_ref, owner_ref, hidden_ref, out_ref, wide_ref
+):
+    hidden = jnp.concatenate(
+        [
+            base_ref[...] + far_ref[...].astype(jnp.float32)
+            for base_ref, far_ref in ((base0_ref, far0_ref), (base1_ref, far1_ref))
+        ],
+        axis=1,
+    ).astype(jnp.bfloat16)
     hidden_ref[...] = hidden
     h = hidden.astype(jnp.float32)
     mean = jnp.mean(h * h, axis=1, keepdims=True)
@@ -322,7 +358,7 @@
         lax.ppermute(qs, "wide", [(i, i ^ flip) for i in devices]) for flip in FLIPS
     ]
     short_in = (queries, key_rows, value_rows, segments)
-    send, keep_short = project(
+    send, keep_short, _ = project(
         short_rows, core_after, short_in, [whole(x) for x in short_in], out_weight
     )
     near_short = lax.ppermute(send, "narrow", across)
@@ -354,18 +390,25 @@
         compiler_params=ROOM,
     )(wide, span_map, *map(in_vmem, queries_by), in_vmem(kv))
     got = exchange(parts, QUERY_GROUPS)
-    send, keep = project(merged_rows, core, (in_vmem(got),), [vmem], out_weight)
+    send, keep, placed = project(merged_rows, core, (in_vmem(got),), [vmem], out_weight, parts=2)
     near = lax.ppermute(send, "narrow", across)
-    pair, keep, near = lax.optimization_barrier((pair_sum(keep, near), keep, near))
-    far = lax.ppermute(pair, "narrow", [(2, 0), (3, 1)])
-    long = keep.astype(jnp.float32) + near.astype(jnp.float32)
-    base = residual.astype(jnp.float32) + jnp.where(level[0] == 0, long, short)
+    send_rest, keep_rest = project_rest(placed, out_weight)
+    near_rest = lax.ppermute(send_rest, "narrow", across)
+    bases, fars = [], []
+    for part, (k, n) in enumerate(((keep, near), (keep_rest, near_rest))):
+        pair, k, n = lax.optimization_barrier((pair_sum(k, n), k, n))
+        fars.append(lax.ppermute(pair, "narrow", [(2, 0), (3, 1)]))
+        at = slice(part * width // 2, (part + 1) * width // 2)
+        long = k.astype(jnp.float32) + n.astype(jnp.float32)
+        bases.append(
+            residual[:, at].astype(jnp.float32) + jnp.where(level[0] == 0, long, short[:, at])
+        )
     rows = residual.shape[0]
     owners = 64
     tiles = 2 * width // HEAD
     hidden, outgoing = pl.pallas_call(
         route_kernel,
-        in_specs=[vmem] * 4,
+        in_specs=[vmem] * 6,
         out_shape=(
             jax.ShapeDtypeStruct((rows, width), bf),
             jax.ShapeDtypeStruct((owners * tiles, HEAD), bf),
@@ -373,7 +416,7 @@
         scratch_shapes=[pltpu.VMEM((owners * tiles, HEAD), jnp.float32)],
         name="route",
         compiler_params=ROOM,
-    )(in_vmem(base), in_vmem(far), norm_gain.reshape(1, width), row_owner)
+    )(*map(in_vmem, bases), *map(in_vmem, fars), norm_gain.reshape(1, width), row_owner)
     arrived = exchange(outgoing.reshape(owners, tiles, HEAD))
     return (hidden, arrived.reshape(1, 1, owners, 2, width))
 

time: 154 us -> 156 us (1.013)
  starting transfers between devices: 33 us -> 36.9 us
  waiting for transfers between devices: 35.9 us -> 34 us
    ppermute x1 -> x3, starting transfers between devices: 1.29 us -> 4.98 us  [the longest x2 2.58 us: on_device(): fars.append(lax.ppermute(pair, 'narrow', [(2, 0), (3, 1)]))]
    pallas_call x1 -> x2, Pallas kernels: 1.82 us -> 4.45 us  [the longest x1 2.63 us: project_rest(): pl.pallas_call(rest_kernel, grid=(width // block,), in_specs=[pl.BlockSpe...]
    ppermute x1, waiting for transfers between devices: 1.95 us -> 0.01 us  [on_device(): near = lax.ppermute(send, 'narrow', across)]
    pallas_call x2, Pallas kernels: 9.9 us -> 8 us  [project(): pl.pallas_call(projector(make_rows), grid_spec=pltpu.PrefetchScalarGridSp...]
    ppermute x1 -> x3, waiting for transfers between devices: 16.5 us -> 16.1 us  [the longest x2 14.9 us: on_device(): fars.append(lax.ppermute(pair, 'narrow', [(2, 0), (3, 1)]))]
  transfers between devices with their start and end apart: 8 -> 10, of which waited for: 6 -> 7; matrix products, arithmetic and copies ran while one was open for 3% -> 3% of each run, Pallas kernels for 0% -> 2%
where the time goes in v5:
time: 156 us
  blocking collectives  55.2 us (35%)
  starting transfers between devices  36.9 us (24%)
  waiting for transfers between devices  34 us (22%)
  Pallas kernels  22.7 us (15%)
  other arithmetic  4.87 us (3%)
    all_to_all x2, blocking collectives, exchange(): return lax.all_to_all(x, 'wide', 0, 0, tiled=True, axis_index_groups=groups)  55.2 us
    all_to_all x1, starting transfers between devices, exchange(): return lax.all_to_all(x, 'wide', 0, 0, tiled=True, axis_index_groups=groups)  16.2 us
    ppermute x3, waiting for transfers between devices, on_device(): lax.ppermute(qs, 'wide', [(i, i ^ flip) for i in devices])  15.2 us
    ppermute x2, waiting for transfers between devices, on_device(): fars.append(lax.ppermute(pair, 'narrow', [(2, 0), (3, 1)]))  14.9 us
    ppermute x3, starting transfers between devices, on_device(): lax.ppermute(qs, 'wide', [(i, i ^ flip) for i in devices])  9.2 us
    pallas_call x1, Pallas kernels, on_device(): pl.pallas_call(attend_kernel, grid_spec=pltpu.PrefetchScalarGridSpec(num_...  8.12 us
    pallas_call x2, Pallas kernels, project(): pl.pallas_call(projector(make_rows), grid_spec=pltpu.PrefetchScalarGridSp...  8 us
  transfers between devices with their start and end apart: 10, of which 7 were waited for; matrix products, arithmetic and copies ran while one was open for 3% of the time, Pallas kernels for 2%

profile of v5, /device:TPU:32, one launch (start us, length us, event | category | flops | bytes accessed | tf_op | source)
XLA Modules:
  0.0 155.7 jit_solution(5907295214118700610)
XLA Ops:
  0.6 2.2 %prep.1 = (bf16[16,128,256]{2,1,0:T(8,128)(2,1)}, bf16[128,512]{1,0:T(8,128)(2,1)}) custom-call(bf16[256,512]{1,0:T(8,128)(2,1)} %refs_0_.1, bf16[256,128]{1,0:T(8,128)(2,1)} %refs_1_.2, bf16[256,128]{1,0:T(8,128)(2,1)} %refs_2_.1), custom_call_target="tpu_custom_call" | custom-call | tf_op jit(solution)/shard_map/prep/pallas_call | solution.py:339
  2.8 5.2 %shard_map.104 = (bf16[64,4096]{1,0:T(8,128)(2,1)}, bf16[64,4096]{1,0:T(8,128)(2,1)}, bf16[128,512]{1,0:T(8,128)(2,1)}) custom-call(s32[1]{0:T(128)} %bitcast.core_ref, bf16[256,512]{1,0:T(8,128)(2,1)} %refs_0_.1, bf16[256,128]{1,0:T(8,128)(2,1)} %refs_1_.2, bf16[256,128]{1,0:T(8,128)(2,1)} %refs_2_.1, s32[1,128]{1,0:T(1,128)} %refs_3_.1, ...), custom_call_target="tpu_custom_call" | custom-call | tf_op jit(solution)/shard_map/pallas_call | solution.py:239
  8.0 2.0 %collective-permute-start = (bf16[64,4096]{1,0:T(8,128)(2,1)}, bf16[64,4096]{1,0:T(8,128)(2,1)S(1)}, u32[]{:S(2)}, u32[]{:S(2)}) collective-permute-start(bf16[64,4096]{1,0:T(8,128)(2,1)} %get-tuple-element.28), channel_id=1, source_target_pairs={{0,4},{4,0},{8,12},{12,8},{1,5},{5,1},{9,13},{13,9},{2,6},{6,2},{1... | collective-permute-start | bytes 1572872 | tf_op jit(solution)/shard_map/ppermute | solution.py:364
  10.0 16.2 %all-to-all-start = ((bf16[16,128,256]{2,1,0:T(8,128)(2,1)}), bf16[16,128,256]{2,1,0:T(8,128)(2,1)S(1)}, u32[]{:S(2)}, u32[]{:S(2)}) async-start(bf16[16,128,256]{2,1,0:T(8,128)(2,1)} %get-tuple-element.31), calls=%async_computation | async-start | bytes 2097152 | tf_op jit(solution)/shard_map/all_to_all | solution.py:325
  27.4 2.4 %collective-permute-start.1 = (bf16[64,4096]{1,0:T(8,128)(2,1)S(1)}, bf16[64,4096]{1,0:T(8,128)(2,1)}, u32[]{:S(2)}, u32[]{:S(2)}) collective-permute-start(bf16[64,4096]{1,0:T(8,128)(2,1)S(1)} %fusion), channel_id=1, source_target_pairs={{0,8},{4,12},{1,9},{5,13},{2,10},{6,14},{3,11},{7,15},{16,24},{20,... | collective-permute-start | bytes 1572872 | tf_op jit(solution)/shard_map/ppermute | solution.py:366
  29.8 2.5 %collective-permute-start.2 = (bf16[128,512]{1,0:T(8,128)(2,1)S(1)}, bf16[128,512]{1,0:T(8,128)(2,1)S(1)}, u32[]{:S(2)}, u32[]{:S(2)}) collective-permute-start(bf16[128,512]{1,0:T(8,128)(2,1)S(1)} %copy-done), channel_id=1, source_target_pairs={{0,16},{16,0},{32,48},{48,32},{64,80},{80,64},{96,112},{112,96},{1... | collective-permute-start | bytes 393224 | tf_op jit(solution)/shard_map/ppermute | solution.py:358
  32.3 2.7 %collective-permute-start.3 = (bf16[128,512]{1,0:T(8,128)(2,1)S(1)}, bf16[128,512]{1,0:T(8,128)(2,1)S(1)}, u32[]{:S(2)}, u32[]{:S(2)}) collective-permute-start(bf16[128,512]{1,0:T(8,128)(2,1)S(1)} %copy-done), channel_id=1, source_target_pairs={{0,128},{16,144},{32,160},{48,176},{64,192},{80,208},{96,224},{112... | collective-permute-start | bytes 393224 | tf_op jit(solution)/shard_map/ppermute | solution.py:358
  35.0 4.0 %collective-permute-start.4 = (bf16[128,512]{1,0:T(8,128)(2,1)S(1)}, bf16[128,512]{1,0:T(8,128)(2,1)S(1)}, u32[]{:S(2)}, u32[]{:S(2)}) collective-permute-start(bf16[128,512]{1,0:T(8,128)(2,1)S(1)} %copy-done), channel_id=1, source_target_pairs={{0,144},{16,128},{32,176},{48,160},{64,208},{80,192},{96,240},{112... | collective-permute-start | bytes 393224 | tf_op jit(solution)/shard_map/ppermute | solution.py:358
  39.0 1.5 collective-permute-done.1
  40.5 1.4 convert_add_fusion
  41.9 12.5 %collective-permute-done.2.q1_ref = bf16[128,512]{1,0:T(8,128)(2,1)S(1)} collective-permute-done((bf16[128,512]{1,0:T(8,128)(2,1)S(1)}, bf16[128,512]{1,0:T(8,128)(2,1)S(1)}, u32[]{:S(2)}, u32[]{:S(2)}) %collective-permute-start.2) | collective-permute-done | bytes 131104 | tf_op jit(solution)/shard_map/ppermute | solution.py:358
  54.4 2.7 %collective-permute-done.4.q3_ref = bf16[128,512]{1,0:T(8,128)(2,1)S(1)} collective-permute-done((bf16[128,512]{1,0:T(8,128)(2,1)S(1)}, bf16[128,512]{1,0:T(8,128)(2,1)S(1)}, u32[]{:S(2)}, u32[]{:S(2)}) %collective-permute-start.4) | collective-permute-done | bytes 131104 | tf_op jit(solution)/shard_map/ppermute | solution.py:358
  58.3 8.1 %attend.1 = bf16[4,144,512]{2,1,0:T(8,128)(2,1)S(1)} custom-call(s32[1]{0:T(128)} %bitcast.1.wide_ref, s32[64]{0:T(128)S(1)} %copy-done.1, bf16[128,512]{1,0:T(8,128)(2,1)S(1)} %copy-done, bf16[128,512]{1,0:T(8,128)(2,1)S(1)} %collective-permute-done.2.q1_ref, bf16[128,512]{1,0:T(8,128)(2,1)S(1)} %collective-permute-done.3.q2_ref, ...), custom_call_target="tpu_custom_call" | custom-call | tf_op jit(solution)/shard_map/attend/pallas_call | solution.py:371
  66.4 11.9 %all_to_all.15.refs_0_ = bf16[4,144,512]{2,1,0:T(8,128)(2,1)S(1)} all-to-all(bf16[4,144,512]{2,1,0:T(8,128)(2,1)S(1)} %attend.1), channel_id=1, replica_groups={{0,16,128,144},{32,48,160,176},{64,80,192,208},{96,112,224,240},{256,27..., dimensions={0} | all-to-all | bytes 1179648 | tf_op jit(solution)/shard_map/all_to_all | solution.py:325
  78.3 2.8 %shard_map.105 = (bf16[64,2048]{1,0:T(8,128)(2,1)}, bf16[64,2048]{1,0:T(8,128)(2,1)}, bf16[128,512]{1,0:T(8,128)(2,1)}) custom-call(s32[1]{0:T(128)} %bitcast.core_ref, bf16[4,144,512]{2,1,0:T(8,128)(2,1)S(1)} %all_to_all.15.refs_0_, bf16[512,4096]{1,0:T(8,128)(2,1)} %weight_ref.1), custom_call_target="tpu_custom_call" | custom-call | tf_op jit(solution)/shard_map/pallas_call | solution.py:239
  81.1 2.0 %collective-permute-start.5 = (bf16[64,2048]{1,0:T(8,128)(2,1)}, bf16[64,2048]{1,0:T(8,128)(2,1)S(1)}, u32[]{:S(2)}, u32[]{:S(2)}) collective-permute-start(bf16[64,2048]{1,0:T(8,128)(2,1)} %get-tuple-element.33), channel_id=1, source_target_pairs={{0,4},{4,0},{8,12},{12,8},{1,5},{5,1},{9,13},{13,9},{2,6},{6,2},{1... | collective-permute-start | bytes 786440 | tf_op jit(solution)/shard_map/ppermute | solution.py:394
  83.3 2.6 %rest.1 = (bf16[64,2048]{1,0:T(8,128)(2,1)}, bf16[64,2048]{1,0:T(8,128)(2,1)}) custom-call(bf16[128,512]{1,0:T(8,128)(2,1)} %get-tuple-element.37.rows_ref, bf16[512,4096]{1,0:T(8,128)(2,1)} %weight_ref.1), custom_call_target="tpu_custom_call" | custom-call | tf_op jit(solution)/shard_map/rest/pallas_call | solution.py:269
  85.9 2.4 %collective-permute-start.6 = (bf16[64,2048]{1,0:T(8,128)(2,1)}, bf16[64,2048]{1,0:T(8,128)(2,1)S(1)}, u32[]{:S(2)}, u32[]{:S(2)}) collective-permute-start(bf16[64,2048]{1,0:T(8,128)(2,1)} %get-tuple-element.39), channel_id=1, source_target_pairs={{0,4},{4,0},{8,12},{12,8},{1,5},{5,1},{9,13},{13,9},{2,6},{6,2},{1... | collective-permute-start | bytes 786440 | tf_op jit(solution)/shard_map/ppermute | solution.py:396
  90.7 1.3 collective-permute-start.7
  92.0 1.3 collective-permute-start.8
  94.6 9.6 %collective-permute-done.7.far0_ref = bf16[64,2048]{1,0:T(8,128)(2,1)S(1)} collective-permute-done((bf16[64,2048]{1,0:T(8,128)(2,1)S(1)}, bf16[64,2048]{1,0:T(8,128)(2,1)S(1)}, u32[]{:S(2)}, u32[]{:S(2)}) %collective-permute-start.7) | collective-permute-done | bytes 262176 | tf_op jit(solution)/shard_map/ppermute | solution.py:400
  104.1 5.3 %collective-permute-done.8.far1_ref = bf16[64,2048]{1,0:T(8,128)(2,1)S(1)} collective-permute-done((bf16[64,2048]{1,0:T(8,128)(2,1)S(1)}, bf16[64,2048]{1,0:T(8,128)(2,1)S(1)}, u32[]{:S(2)}, u32[]{:S(2)}) %collective-permute-start.8) | collective-permute-done | bytes 262176 | tf_op jit(solution)/shard_map/ppermute | solution.py:400
  109.5 1.8 %route.1 = (bf16[64,4096]{1,0:T(8,128)(2,1)}, bf16[4096,128]{1,0:T(8,128)(2,1)S(1)}) custom-call(f32[64,2048]{1,0:T(8,128)S(1)} %get-tuple-element.47.base0_ref, f32[64,2048]{1,0:T(8,128)S(1)} %get-tuple-element.46.base1_ref, bf16[64,2048]{1,0:T(8,128)(2,1)S(1)} %collective-permute-done.7.far0_ref, bf16[64,2048]{1,0:T(8,128)(2,1)S(1)} %collective-permute-done.8.far1_ref, ...), custom_call_target="tpu_custom_call" | custom-call | tf_op jit(solution)/shard_map/route/pallas_call | solution.py:409
  111.3 43.3 %all_to_all.16 = bf16[64,64,128]{2,1,0:T(8,128)(2,1)S(1)} all-to-all(bf16[64,64,128]{2,1,0:T(8,128)(2,1)S(1)} %bitcast.3), channel_id=1, replica_groups=mesh['wide'=64,'narrow'=4,'rep'=4] {'wide'}, dimensions={0} | all-to-all | bytes 2097152 | tf_op jit(solution)/shard_map/all_to_all | solution.py:325
  (24 shorter events, 7.1 us)
Async XLA Ops:
  2.8 27.0 %copy-start = (bf16[128,512]{1,0:T(8,128)(2,1)S(1)}, bf16[128,512]{1,0:T(8,128)(2,1)}, u32[]{:S(2)}) copy-start(bf16[128,512]{1,0:T(8,128)(2,1)} %get-tuple-element.30.q0_ref) | copy-start | bytes 393220
  8.0 50.3 %copy-start.1 = (s32[64]{0:T(128)S(1)}, s32[64]{0:T(128)}, u32[]{:S(2)}) copy-start(s32[64]{0:T(128)} %span_ref.1) | copy-start | bytes 772
  8.0 18.3 %collective-permute-start = (bf16[64,4096]{1,0:T(8,128)(2,1)}, bf16[64,4096]{1,0:T(8,128)(2,1)S(1)}, u32[]{:S(2)}, u32[]{:S(2)}) collective-permute-start(bf16[64,4096]{1,0:T(8,128)(2,1)} %get-tuple-element.28), channel_id=1, source_target_pairs={{0,4},{4,0},{8,12},{12,8},{1,5},{5,1},{9,13},{13,9},{2,6},{6,2},{1... | collective-permute-start | bytes 1572872 | tf_op jit(solution)/shard_map/ppermute | solution.py:364
  10.0 48.2 %all-to-all-start = ((bf16[16,128,256]{2,1,0:T(8,128)(2,1)}), bf16[16,128,256]{2,1,0:T(8,128)(2,1)S(1)}, u32[]{:S(2)}, u32[]{:S(2)}) async-start(bf16[16,128,256]{2,1,0:T(8,128)(2,1)} %get-tuple-element.31), calls=%async_computation | async-start | bytes 2097152 | tf_op jit(solution)/shard_map/all_to_all | solution.py:325
  27.4 13.1 %collective-permute-start.1 = (bf16[64,4096]{1,0:T(8,128)(2,1)S(1)}, bf16[64,4096]{1,0:T(8,128)(2,1)}, u32[]{:S(2)}, u32[]{:S(2)}) collective-permute-start(bf16[64,4096]{1,0:T(8,128)(2,1)S(1)} %fusion), channel_id=1, source_target_pairs={{0,8},{4,12},{1,9},{5,13},{2,10},{6,14},{3,11},{7,15},{16,24},{20,... | collective-permute-start | bytes 1572872 | tf_op jit(solution)/shard_map/ppermute | solution.py:366
  29.8 24.6 %collective-permute-start.2 = (bf16[128,512]{1,0:T(8,128)(2,1)S(1)}, bf16[128,512]{1,0:T(8,128)(2,1)S(1)}, u32[]{:S(2)}, u32[]{:S(2)}) collective-permute-start(bf16[128,512]{1,0:T(8,128)(2,1)S(1)} %copy-done), channel_id=1, source_target_pairs={{0,16},{16,0},{32,48},{48,32},{64,80},{80,64},{96,112},{112,96},{1... | collective-permute-start | bytes 393224 | tf_op jit(solution)/shard_map/ppermute | solution.py:358
  32.3 22.1 %collective-permute-start.3 = (bf16[128,512]{1,0:T(8,128)(2,1)S(1)}, bf16[128,512]{1,0:T(8,128)(2,1)S(1)}, u32[]{:S(2)}, u32[]{:S(2)}) collective-permute-start(bf16[128,512]{1,0:T(8,128)(2,1)S(1)} %copy-done), channel_id=1, source_target_pairs={{0,128},{16,144},{32,160},{48,176},{64,192},{80,208},{96,224},{112... | collective-permute-start | bytes 393224 | tf_op jit(solution)/shard_map/ppermute | solution.py:358
  35.0 22.1 %collective-permute-start.4 = (bf16[128,512]{1,0:T(8,128)(2,1)S(1)}, bf16[128,512]{1,0:T(8,128)(2,1)S(1)}, u32[]{:S(2)}, u32[]{:S(2)}) collective-permute-start(bf16[128,512]{1,0:T(8,128)(2,1)S(1)} %copy-done), channel_id=1, source_target_pairs={{0,144},{16,128},{32,176},{48,160},{64,208},{80,192},{96,240},{112... | collective-permute-start | bytes 393224 | tf_op jit(solution)/shard_map/ppermute | solution.py:358
  41.9 41.3 %copy-start.5 = (s32[64,1]{0,1:T(1,128)S(1)}, s32[64,1]{0,1:T(1,128)}, u32[]{:S(2)}) copy-start(s32[64,1]{0,1:T(1,128)} %param.17) | copy-start | bytes 772
  41.9 41.4 %copy-start.4 = (bf16[4096]{0:T(1024)(128)(2,1)S(1)}, bf16[4096]{0:T(1024)(128)(2,1)}, u32[]{:S(2)}) copy-start(bf16[4096]{0:T(1024)(128)(2,1)} %param.14) | copy-start | bytes 24580
  78.3 15.0 %copy-start.3 = (bf16[64,4096]{1,0:T(8,128)(2,1)S(1)}, bf16[64,4096]{1,0:T(8,128)(2,1)}, u32[]{:S(2)}) copy-start(bf16[64,4096]{1,0:T(8,128)(2,1)} %param.12) | copy-start | bytes 1572868
  81.1 7.2 %copy-start.2 = (bf16[64,2048]{1,0:T(8,128)(2,1)S(1)}, bf16[64,2048]{1,0:T(8,128)(2,1)}, u32[]{:S(2)}) copy-start(bf16[64,2048]{1,0:T(8,128)(2,1)} %get-tuple-element.34) | copy-start | bytes 786436
  81.1 7.2 %collective-permute-start.5 = (bf16[64,2048]{1,0:T(8,128)(2,1)}, bf16[64,2048]{1,0:T(8,128)(2,1)S(1)}, u32[]{:S(2)}, u32[]{:S(2)}) collective-permute-start(bf16[64,2048]{1,0:T(8,128)(2,1)} %get-tuple-element.33), channel_id=1, source_target_pairs={{0,4},{4,0},{8,12},{12,8},{1,5},{5,1},{9,13},{13,9},{2,6},{6,2},{1... | collective-permute-start | bytes 786440 | tf_op jit(solution)/shard_map/ppermute | solution.py:394
  85.9 3.8 %collective-permute-start.6 = (bf16[64,2048]{1,0:T(8,128)(2,1)}, bf16[64,2048]{1,0:T(8,128)(2,1)S(1)}, u32[]{:S(2)}, u32[]{:S(2)}) collective-permute-start(bf16[64,2048]{1,0:T(8,128)(2,1)} %get-tuple-element.39), channel_id=1, source_target_pairs={{0,4},{4,0},{8,12},{12,8},{1,5},{5,1},{9,13},{13,9},{2,6},{6,2},{1... | collective-permute-start | bytes 786440 | tf_op jit(solution)/shard_map/ppermute | solution.py:396
  90.7 13.4 %collective-permute-start.7 = (bf16[64,2048]{1,0:T(8,128)(2,1)S(1)}, bf16[64,2048]{1,0:T(8,128)(2,1)S(1)}, u32[]{:S(2)}, u32[]{:S(2)}) collective-permute-start(bf16[64,2048]{1,0:T(8,128)(2,1)S(1)} %add_convert_fusion.1), channel_id=1, source_target_pairs={{8,0},{12,4},{9,1},{13,5},{10,2},{14,6},{11,3},{15,7},{24,16},{28,... | collective-permute-start | bytes 786440 | tf_op jit(solution)/shard_map/ppermute | solution.py:400
  92.0 17.4 %collective-permute-start.8 = (bf16[64,2048]{1,0:T(8,128)(2,1)S(1)}, bf16[64,2048]{1,0:T(8,128)(2,1)S(1)}, u32[]{:S(2)}, u32[]{:S(2)}) collective-permute-start(bf16[64,2048]{1,0:T(8,128)(2,1)S(1)} %add_convert_fusion), channel_id=1, source_target_pairs={{8,0},{12,4},{9,1},{13,5},{10,2},{14,6},{11,3},{15,7},{24,16},{28,... | collective-permute-start | bytes 786440 | tf_op jit(solution)/shard_map/ppermute | solution.py:400

commit v6 on v5

--- a/solution.py
+++ b/solution.py
@@ -51,10 +51,10 @@
 
 
 def prep_kernel(q_ref, k_ref, v_ref, kv_out, q_out):
-    kv = jnp.concatenate([k_ref[:LONG_DEV], v_ref[:LONG_DEV].T], axis=1)
+    kv = jnp.concatenate([k_ref[...], v_ref[...].T], axis=1)
     for i in range(kv_out.shape[0]):
         kv_out[i] = kv
-    q_out[...] = heads_across(q_ref[:LONG_DEV])
+    q_out[...] = heads_across(q_ref[...])
 
 
 def short_rows(q_ref, k_ref, v_ref, seg_ref):
@@ -339,7 +339,10 @@
     kv, qs = pl.pallas_call(
         prep_kernel,
         grid=(1,),
-        in_specs=[whole(x) for x in (queries, key_rows, value_rows)],
+        in_specs=[
+            pl.BlockSpec((LONG_DEV, x.shape[1]), lambda i: (0, 0))
+            for x in (queries, key_rows, value_rows)
+        ],
         out_specs=(
             pl.BlockSpec((16, LONG_DEV, 2 * HEAD), lambda i: (0, 0, 0)),
             pl.BlockSpec((LONG_DEV, cols), lambda i: (0, 0)),
@@ -354,9 +357,9 @@
     kv, qs, core_after = lax.optimization_barrier((kv, qs, core))
     kv = exchange(kv, KEY_GROUPS)
     devices = range(SIDE * SIDE)
-    queries_by = [qs] + [
-        lax.ppermute(qs, "wide", [(i, i ^ flip) for i in devices]) for flip in FLIPS
-    ]
+    queries_by = [qs]
+    for flip in FLIPS:
+        queries_by.append(lax.ppermute(qs, "wide", [(i, i ^ flip) for i in devices]))
     short_in = (queries, key_rows, value_rows, segments)
     send, keep_short, _ = project(
         short_rows, core_after, short_in, [whole(x) for x in short_in], out_weight
@@ -367,7 +370,6 @@
     short = (keep_short.astype(jnp.float32) + near_short.astype(jnp.float32)) + far_short.astype(
         jnp.float32
     )
-    wide, short = lax.optimization_barrier((wide, short))
     parts = pl.pallas_call(
         attend_kernel,
         grid_spec=pltpu.PrefetchScalarGridSpec(

time: 156 us -> 146 us (0.936)
  the two profiles are of different devices: /device:TPU:32 before, /device:TPU:288 now
where the time goes in v6:
time: 146 us; the launch traced here: 145 us
  starting transfers between devices  44.1 us (30%)
  blocking collectives  40.5 us (28%)
  waiting for transfers between devices  32.2 us (22%)
  Pallas kernels  23.8 us (16%)
  other arithmetic  2.7 us (2%)
    all_to_all x1, blocking collectives, exchange(): return lax.all_to_all(x, 'wide', 0, 0, tiled=True, axis_index_groups=groups)  40.5 us
    all_to_all x2, starting transfers between devices, exchange(): return lax.all_to_all(x, 'wide', 0, 0, tiled=True, axis_index_groups=groups)  21 us
    ppermute x3, waiting for transfers between devices, on_device(): lax.ppermute(qs, 'wide', [(i, i ^ flip) for i in devices])  15.9 us
    ppermute x2, waiting for transfers between devices, on_device(): fars.append(lax.ppermute(pair, 'narrow', [(2, 0), (3, 1)]))  13.9 us
    pallas_call x1, Pallas kernels, on_device(): pl.pallas_call(attend_kernel, grid_spec=pltpu.PrefetchScalarGridSpec(num_...  9.32 us
    ppermute x3, starting transfers between devices, on_device(): lax.ppermute(qs, 'wide', [(i, i ^ flip) for i in devices])  9.21 us
    pallas_call x2, Pallas kernels, project(): pl.pallas_call(projector(make_rows), grid_spec=pltpu.PrefetchScalarGridSp...  7.9 us
    ppermute x1, starting transfers between devices, on_device(): far_short = lax.ppermute(pair_short, 'narrow', [(0, 2), (1, 3)])  5.22 us
  transfers between devices with their start and end apart: 11, of which 7 were waited for; matrix products, arithmetic and copies ran while one was open for 2% of the time, Pallas kernels for 14%

profile of v6, /device:TPU:288, one launch (start us, length us, event | category | flops | bytes accessed | tf_op | source)
XLA Modules:
  0.0 145.4 jit_solution(1628372602871207196)
XLA Ops:
  0.6 2.1 %prep.1 = (bf16[16,128,256]{2,1,0:T(8,128)(2,1)}, bf16[128,512]{1,0:T(8,128)(2,1)}) custom-call(bf16[256,512]{1,0:T(8,128)(2,1)} %refs_0_.1, bf16[256,128]{1,0:T(8,128)(2,1)} %refs_1_.3, bf16[256,128]{1,0:T(8,128)(2,1)} %refs_2_.1), custom_call_target="tpu_custom_call" | custom-call | tf_op jit(solution)/shard_map/prep/pallas_call | solution.py:339
  2.7 12.7 %all-to-all-start = ((bf16[16,128,256]{2,1,0:T(8,128)(2,1)}), bf16[16,128,256]{2,1,0:T(8,128)(2,1)S(1)}, u32[]{:S(2)}, u32[]{:S(2)}) async-start(bf16[16,128,256]{2,1,0:T(8,128)(2,1)} %get-tuple-element.25), calls=%async_computation | async-start | bytes 2097152 | tf_op jit(solution)/shard_map/all_to_all | solution.py:325
  15.5 5.1 %shard_map.105 = (bf16[64,4096]{1,0:T(8,128)(2,1)}, bf16[64,4096]{1,0:T(8,128)(2,1)}, bf16[128,512]{1,0:T(8,128)(2,1)}) custom-call(s32[1]{0:T(128)} %bitcast.core_ref, bf16[256,512]{1,0:T(8,128)(2,1)} %refs_0_.1, bf16[256,128]{1,0:T(8,128)(2,1)} %refs_1_.3, bf16[256,128]{1,0:T(8,128)(2,1)} %refs_2_.1, s32[1,128]{1,0:T(1,128)} %refs_3_.1, ...), custom_call_target="tpu_custom_call" | custom-call | tf_op jit(solution)/shard_map/pallas_call | solution.py:239
  20.6 1.9 %collective-permute-start.4 = (bf16[64,4096]{1,0:T(8,128)(2,1)}, bf16[64,4096]{1,0:T(8,128)(2,1)S(1)}, u32[]{:S(2)}, u32[]{:S(2)}) collective-permute-start(bf16[64,4096]{1,0:T(8,128)(2,1)} %get-tuple-element.32), channel_id=1, source_target_pairs={{0,4},{4,0},{8,12},{12,8},{1,5},{5,1},{9,13},{13,9},{2,6},{6,2},{1... | collective-permute-start | bytes 1572872 | tf_op jit(solution)/shard_map/ppermute | solution.py:367
  22.5 2.5 %collective-permute-start = (bf16[128,512]{1,0:T(8,128)(2,1)S(1)}, bf16[128,512]{1,0:T(8,128)(2,1)S(1)}, u32[]{:S(2)}, u32[]{:S(2)}) collective-permute-start(bf16[128,512]{1,0:T(8,128)(2,1)S(1)} %copy-done), channel_id=1, source_target_pairs={{0,16},{16,0},{32,48},{48,32},{64,80},{80,64},{96,112},{112,96},{1... | collective-permute-start | bytes 393224 | tf_op jit(solution)/shard_map/ppermute | solution.py:362
  25.0 2.7 %collective-permute-start.1 = (bf16[128,512]{1,0:T(8,128)(2,1)S(1)}, bf16[128,512]{1,0:T(8,128)(2,1)S(1)}, u32[]{:S(2)}, u32[]{:S(2)}) collective-permute-start(bf16[128,512]{1,0:T(8,128)(2,1)S(1)} %copy-done), channel_id=1, source_target_pairs={{0,128},{16,144},{32,160},{48,176},{64,192},{80,208},{96,224},{112... | collective-permute-start | bytes 393224 | tf_op jit(solution)/shard_map/ppermute | solution.py:362
  27.8 4.0 %collective-permute-start.2 = (bf16[128,512]{1,0:T(8,128)(2,1)S(1)}, bf16[128,512]{1,0:T(8,128)(2,1)S(1)}, u32[]{:S(2)}, u32[]{:S(2)}) collective-permute-start(bf16[128,512]{1,0:T(8,128)(2,1)S(1)} %copy-done), channel_id=1, source_target_pairs={{0,144},{16,128},{32,176},{48,160},{64,208},{80,192},{96,240},{112... | collective-permute-start | bytes 393224 | tf_op jit(solution)/shard_map/ppermute | solution.py:362
  31.8 13.6 %collective-permute-done.q1_ref = bf16[128,512]{1,0:T(8,128)(2,1)S(1)} collective-permute-done((bf16[128,512]{1,0:T(8,128)(2,1)S(1)}, bf16[128,512]{1,0:T(8,128)(2,1)S(1)}, u32[]{:S(2)}, u32[]{:S(2)}) %collective-permute-start) | collective-permute-done | bytes 131104 | tf_op jit(solution)/shard_map/ppermute | solution.py:362
  45.4 2.3 %collective-permute-done.1.q2_ref = bf16[128,512]{1,0:T(8,128)(2,1)S(1)} collective-permute-done((bf16[128,512]{1,0:T(8,128)(2,1)S(1)}, bf16[128,512]{1,0:T(8,128)(2,1)S(1)}, u32[]{:S(2)}, u32[]{:S(2)}) %collective-permute-start.1) | collective-permute-done | bytes 131104 | tf_op jit(solution)/shard_map/ppermute | solution.py:362
  47.7 9.3 %attend.1 = bf16[4,144,512]{2,1,0:T(8,128)(2,1)} custom-call(s32[1]{0:T(128)} %bitcast.1.wide_ref, s32[64]{0:T(128)S(1)} %copy-done.1, bf16[128,512]{1,0:T(8,128)(2,1)S(1)} %copy-done, bf16[128,512]{1,0:T(8,128)(2,1)S(1)} %collective-permute-done.q1_ref, bf16[128,512]{1,0:T(8,128)(2,1)S(1)} %collective-permute-done.1.q2_ref, ...), custom_call_target="tpu_custom_call" | custom-call | tf_op jit(solution)/shard_map/attend/pallas_call | solution.py:373
  57.0 8.3 %all-to-all-start.1 = ((bf16[4,144,512]{2,1,0:T(8,128)(2,1)}), bf16[4,144,512]{2,1,0:T(8,128)(2,1)S(1)}, u32[]{:S(2)}, u32[]{:S(2)}) async-start(bf16[4,144,512]{2,1,0:T(8,128)(2,1)} %attend.1), calls=%async_computation.1 | async-start | bytes 1179648 | tf_op jit(solution)/shard_map/all_to_all | solution.py:325
  65.3 1.2 fusion
  66.4 5.2 %collective-permute-start.5 = (bf16[64,4096]{1,0:T(8,128)(2,1)S(1)}, bf16[64,4096]{1,0:T(8,128)(2,1)S(1)}, u32[]{:S(2)}, u32[]{:S(2)}) collective-permute-start(bf16[64,4096]{1,0:T(8,128)(2,1)S(1)} %fusion), channel_id=1, source_target_pairs={{0,8},{4,12},{1,9},{5,13},{2,10},{6,14},{3,11},{7,15},{16,24},{20,... | collective-permute-start | bytes 1572872 | tf_op jit(solution)/shard_map/ppermute | solution.py:369
  71.8 1.8 %all-to-all-done.1.refs_0_ = bf16[4,144,512]{2,1,0:T(8,128)(2,1)S(1)} async-done(((bf16[4,144,512]{2,1,0:T(8,128)(2,1)}), bf16[4,144,512]{2,1,0:T(8,128)(2,1)S(1)}, u32[]{:S(2)}, u32[]{:S(2)}) %all-to-all-start.1) | async-done | bytes 589856 | tf_op jit(solution)/shard_map/all_to_all | solution.py:325
  73.6 2.8 %shard_map.104 = (bf16[64,2048]{1,0:T(8,128)(2,1)}, bf16[64,2048]{1,0:T(8,128)(2,1)}, bf16[128,512]{1,0:T(8,128)(2,1)}) custom-call(s32[1]{0:T(128)} %bitcast.core_ref, bf16[4,144,512]{2,1,0:T(8,128)(2,1)S(1)} %all-to-all-done.1.refs_0_, bf16[512,4096]{1,0:T(8,128)(2,1)} %weight_ref.1), custom_call_target="tpu_custom_call" | custom-call | tf_op jit(solution)/shard_map/pallas_call | solution.py:239
  76.4 2.7 %rest.1 = (bf16[64,2048]{1,0:T(8,128)(2,1)}, bf16[64,2048]{1,0:T(8,128)(2,1)}) custom-call(bf16[128,512]{1,0:T(8,128)(2,1)} %get-tuple-element.33.rows_ref, bf16[512,4096]{1,0:T(8,128)(2,1)} %weight_ref.1), custom_call_target="tpu_custom_call" | custom-call | tf_op jit(solution)/shard_map/rest/pallas_call | solution.py:269
  79.1 2.0 %collective-permute-start.6 = (bf16[64,2048]{1,0:T(8,128)(2,1)}, bf16[64,2048]{1,0:T(8,128)(2,1)S(1)}, u32[]{:S(2)}, u32[]{:S(2)}) collective-permute-start(bf16[64,2048]{1,0:T(8,128)(2,1)} %get-tuple-element.35), channel_id=1, source_target_pairs={{0,4},{4,0},{8,12},{12,8},{1,5},{5,1},{9,13},{13,9},{2,6},{6,2},{1... | collective-permute-start | bytes 786440 | tf_op jit(solution)/shard_map/ppermute | solution.py:398
  81.6 2.1 %collective-permute-start.3 = (bf16[64,2048]{1,0:T(8,128)(2,1)S(1)}, bf16[64,2048]{1,0:T(8,128)(2,1)S(1)}, u32[]{:S(2)}, u32[]{:S(2)}) collective-permute-start(bf16[64,2048]{1,0:T(8,128)(2,1)S(1)} %copy-done.8), channel_id=1, source_target_pairs={{0,4},{4,0},{8,12},{12,8},{1,5},{5,1},{9,13},{13,9},{2,6},{6,2},{1... | collective-permute-start | bytes 786440 | tf_op jit(solution)/shard_map/ppermute | solution.py:396
  85.1 1.3 collective-permute-start.7
  86.4 1.3 collective-permute-start.8
  88.0 8.6 %collective-permute-done.7.far0_ref = bf16[64,2048]{1,0:T(8,128)(2,1)S(1)} collective-permute-done((bf16[64,2048]{1,0:T(8,128)(2,1)S(1)}, bf16[64,2048]{1,0:T(8,128)(2,1)S(1)}, u32[]{:S(2)}, u32[]{:S(2)}) %collective-permute-start.7) | collective-permute-done | bytes 262176 | tf_op jit(solution)/shard_map/ppermute | solution.py:402
  96.7 5.3 %collective-permute-done.8.far1_ref = bf16[64,2048]{1,0:T(8,128)(2,1)S(1)} collective-permute-done((bf16[64,2048]{1,0:T(8,128)(2,1)S(1)}, bf16[64,2048]{1,0:T(8,128)(2,1)S(1)}, u32[]{:S(2)}, u32[]{:S(2)}) %collective-permute-start.8) | collective-permute-done | bytes 262176 | tf_op jit(solution)/shard_map/ppermute | solution.py:402
  102.0 1.8 %route.1 = (bf16[64,4096]{1,0:T(8,128)(2,1)}, bf16[4096,128]{1,0:T(8,128)(2,1)S(1)}) custom-call(f32[64,2048]{1,0:T(8,128)S(1)} %get-tuple-element.43.base0_ref, f32[64,2048]{1,0:T(8,128)S(1)} %get-tuple-element.42.base1_ref, bf16[64,2048]{1,0:T(8,128)(2,1)S(1)} %collective-permute-done.7.far0_ref, bf16[64,2048]{1,0:T(8,128)(2,1)S(1)} %collective-permute-done.8.far1_ref, ...), custom_call_target="tpu_custom_call" | custom-call | tf_op jit(solution)/shard_map/route/pallas_call | solution.py:411
  103.8 40.5 %all_to_all.15 = bf16[64,64,128]{2,1,0:T(8,128)(2,1)S(1)} all-to-all(bf16[64,64,128]{2,1,0:T(8,128)(2,1)S(1)} %bitcast.3), channel_id=1, replica_groups=mesh['wide'=64,'narrow'=4,'rep'=4] {'wide'}, dimensions={0} | all-to-all | bytes 2097152 | tf_op jit(solution)/shard_map/all_to_all | solution.py:325
  (31 shorter events, 3.4 us)
Async XLA Ops:
  0.6 47.0 %copy-start.1 = (s32[64]{0:T(128)S(1)}, s32[64]{0:T(128)}, u32[]{:S(2)}) copy-start(s32[64]{0:T(128)} %span_ref.1) | copy-start | bytes 772
  2.7 19.8 %copy-start = (bf16[128,512]{1,0:T(8,128)(2,1)S(1)}, bf16[128,512]{1,0:T(8,128)(2,1)}, u32[]{:S(2)}) copy-start(bf16[128,512]{1,0:T(8,128)(2,1)} %get-tuple-element.24.q0_ref) | copy-start | bytes 393220
  2.7 44.9 %all-to-all-start = ((bf16[16,128,256]{2,1,0:T(8,128)(2,1)}), bf16[16,128,256]{2,1,0:T(8,128)(2,1)S(1)}, u32[]{:S(2)}, u32[]{:S(2)}) async-start(bf16[16,128,256]{2,1,0:T(8,128)(2,1)} %get-tuple-element.25), calls=%async_computation | async-start | bytes 2097152 | tf_op jit(solution)/shard_map/all_to_all | solution.py:325
  15.5 56.2 %copy-start.6 = (bf16[4096]{0:T(1024)(128)(2,1)S(1)}, bf16[4096]{0:T(1024)(128)(2,1)}, u32[]{:S(2)}) copy-start(bf16[4096]{0:T(1024)(128)(2,1)} %param.14) | copy-start | bytes 24580
  15.5 56.2 %copy-start.7 = (s32[64,1]{0,1:T(1,128)S(1)}, s32[64,1]{0,1:T(1,128)}, u32[]{:S(2)}) copy-start(s32[64,1]{0,1:T(1,128)} %param.17) | copy-start | bytes 772
  20.6 44.7 %collective-permute-start.4 = (bf16[64,4096]{1,0:T(8,128)(2,1)}, bf16[64,4096]{1,0:T(8,128)(2,1)S(1)}, u32[]{:S(2)}, u32[]{:S(2)}) collective-permute-start(bf16[64,4096]{1,0:T(8,128)(2,1)} %get-tuple-element.32), channel_id=1, source_target_pairs={{0,4},{4,0},{8,12},{12,8},{1,5},{5,1},{9,13},{13,9},{2,6},{6,2},{1... | collective-permute-start | bytes 1572872 | tf_op jit(solution)/shard_map/ppermute | solution.py:367
  22.5 22.9 %collective-permute-start = (bf16[128,512]{1,0:T(8,128)(2,1)S(1)}, bf16[128,512]{1,0:T(8,128)(2,1)S(1)}, u32[]{:S(2)}, u32[]{:S(2)}) collective-permute-start(bf16[128,512]{1,0:T(8,128)(2,1)S(1)} %copy-done), channel_id=1, source_target_pairs={{0,16},{16,0},{32,48},{48,32},{64,80},{80,64},{96,112},{112,96},{1... | collective-permute-start | bytes 393224 | tf_op jit(solution)/shard_map/ppermute | solution.py:362
  25.0 22.6 %collective-permute-start.1 = (bf16[128,512]{1,0:T(8,128)(2,1)S(1)}, bf16[128,512]{1,0:T(8,128)(2,1)S(1)}, u32[]{:S(2)}, u32[]{:S(2)}) collective-permute-start(bf16[128,512]{1,0:T(8,128)(2,1)S(1)} %copy-done), channel_id=1, source_target_pairs={{0,128},{16,144},{32,160},{48,176},{64,192},{80,208},{96,224},{112... | collective-permute-start | bytes 393224 | tf_op jit(solution)/shard_map/ppermute | solution.py:362
  27.8 19.9 %collective-permute-start.2 = (bf16[128,512]{1,0:T(8,128)(2,1)S(1)}, bf16[128,512]{1,0:T(8,128)(2,1)S(1)}, u32[]{:S(2)}, u32[]{:S(2)}) collective-permute-start(bf16[128,512]{1,0:T(8,128)(2,1)S(1)} %copy-done), channel_id=1, source_target_pairs={{0,144},{16,128},{32,176},{48,160},{64,208},{80,192},{96,240},{112... | collective-permute-start | bytes 393224 | tf_op jit(solution)/shard_map/ppermute | solution.py:362
  57.0 16.6 %all-to-all-start.1 = ((bf16[4,144,512]{2,1,0:T(8,128)(2,1)}), bf16[4,144,512]{2,1,0:T(8,128)(2,1)S(1)}, u32[]{:S(2)}, u32[]{:S(2)}) async-start(bf16[4,144,512]{2,1,0:T(8,128)(2,1)} %attend.1), calls=%async_computation.1 | async-start | bytes 1179648 | tf_op jit(solution)/shard_map/all_to_all | solution.py:325
  66.4 15.0 %collective-permute-start.5 = (bf16[64,4096]{1,0:T(8,128)(2,1)S(1)}, bf16[64,4096]{1,0:T(8,128)(2,1)S(1)}, u32[]{:S(2)}, u32[]{:S(2)}) collective-permute-start(bf16[64,4096]{1,0:T(8,128)(2,1)S(1)} %fusion), channel_id=1, source_target_pairs={{0,8},{4,12},{1,9},{5,13},{2,10},{6,14},{3,11},{7,15},{16,24},{20,... | collective-permute-start | bytes 1572872 | tf_op jit(solution)/shard_map/ppermute | solution.py:369
  71.8 9.6 %copy-start.2 = (bf16[64,4096]{1,0:T(8,128)(2,1)S(1)}, bf16[64,4096]{1,0:T(8,128)(2,1)}, u32[]{:S(2)}) copy-start(bf16[64,4096]{1,0:T(8,128)(2,1)} %get-tuple-element.31) | copy-start | bytes 1572868
  76.3 5.2 %copy-start.8 = (bf16[64,2048]{1,0:T(8,128)(2,1)S(1)}, bf16[64,2048]{1,0:T(8,128)(2,1)}, u32[]{:S(2)}) copy-start(bf16[64,2048]{1,0:T(8,128)(2,1)} %get-tuple-element.27) | copy-start | bytes 786436
  76.3 8.7 %copy-start.3 = (bf16[64,2048]{1,0:T(8,128)(2,1)S(1)}, bf16[64,2048]{1,0:T(8,128)(2,1)}, u32[]{:S(2)}) copy-start(bf16[64,2048]{1,0:T(8,128)(2,1)} %get-tuple-element.28) | copy-start | bytes 786436
  76.3 11.4 %copy-start.5 = (bf16[64,4096]{1,0:T(8,128)(2,1)S(1)}, bf16[64,4096]{1,0:T(8,128)(2,1)}, u32[]{:S(2)}) copy-start(bf16[64,4096]{1,0:T(8,128)(2,1)} %param.12) | copy-start | bytes 1572868
  79.1 8.7 %copy-start.4 = (bf16[64,2048]{1,0:T(8,128)(2,1)S(1)}, bf16[64,2048]{1,0:T(8,128)(2,1)}, u32[]{:S(2)}) copy-start(bf16[64,2048]{1,0:T(8,128)(2,1)} %get-tuple-element.36) | copy-start | bytes 786436
  79.1 4.7 %collective-permute-start.6 = (bf16[64,2048]{1,0:T(8,128)(2,1)}, bf16[64,2048]{1,0:T(8,128)(2,1)S(1)}, u32[]{:S(2)}, u32[]{:S(2)}) collective-permute-start(bf16[64,2048]{1,0:T(8,128)(2,1)} %get-tuple-element.35), channel_id=1, source_target_pairs={{0,4},{4,0},{8,12},{12,8},{1,5},{5,1},{9,13},{13,9},{2,6},{6,2},{1... | collective-permute-start | bytes 786440 | tf_op jit(solution)/shard_map/ppermute | solution.py:398
  81.6 3.4 %collective-permute-start.3 = (bf16[64,2048]{1,0:T(8,128)(2,1)S(1)}, bf16[64,2048]{1,0:T(8,128)(2,1)S(1)}, u32[]{:S(2)}, u32[]{:S(2)}) collective-permute-start(bf16[64,2048]{1,0:T(8,128)(2,1)S(1)} %copy-done.8), channel_id=1, source_target_pairs={{0,4},{4,0},{8,12},{12,8},{1,5},{5,1},{9,13},{13,9},{2,6},{6,2},{1... | collective-permute-start | bytes 786440 | tf_op jit(solution)/shard_map/ppermute | solution.py:396
  85.1 11.6 %collective-permute-start.7 = (bf16[64,2048]{1,0:T(8,128)(2,1)S(1)}, bf16[64,2048]{1,0:T(8,128)(2,1)S(1)}, u32[]{:S(2)}, u32[]{:S(2)}) collective-permute-start(bf16[64,2048]{1,0:T(8,128)(2,1)S(1)} %add_convert_fusion.1), channel_id=1, source_target_pairs={{8,0},{12,4},{9,1},{13,5},{10,2},{14,6},{11,3},{15,7},{24,16},{28,... | collective-permute-start | bytes 786440 | tf_op jit(solution)/shard_map/ppermute | solution.py:402
  86.4 15.6 %collective-permute-start.8 = (bf16[64,2048]{1,0:T(8,128)(2,1)S(1)}, bf16[64,2048]{1,0:T(8,128)(2,1)S(1)}, u32[]{:S(2)}, u32[]{:S(2)}) collective-permute-start(bf16[64,2048]{1,0:T(8,128)(2,1)S(1)} %add_convert_fusion), channel_id=1, source_target_pairs={{8,0},{12,4},{9,1},{13,5},{10,2},{14,6},{11,3},{15,7},{24,16},{28,... | collective-permute-start | bytes 786440 | tf_op jit(solution)/shard_map/ppermute | solution.py:402
